TPU v7x, 128 devices: a whole 4x4x4 slice. The times are simulated.
128 devices in a mesh: rep: 1, data: 16 (over z, y), expert: 8 (over x, core).
Axes of the slice: x: 4, y: 4, z: 4, core: 2. Of those that a mesh axis runs over, the one named last changes fastest.
Arguments:
- tok_in: bfloat16 [262144, 512], P(('rep', 'expert', 'data'))
- expert_idx: int32 [262144, 8], P(('rep', 'expert', 'data'))
- gate_wt: float32 [262144, 8], P(('rep', 'expert', 'data'))
- w_gate: bfloat16 [128, 512, 192], P('expert', 'data')
- w_up: bfloat16 [128, 512, 192], P('expert', 'data')
- w_down: bfloat16 [128, 192, 512], P('expert', None, 'data')
- grad_out: bfloat16 [262144, 512], P(('rep', 'expert', 'data'))
Outputs:
- output 1: bfloat16 [262144, 512], P(('rep', 'expert', 'data'))
- output 2: bfloat16 [262144, 512], P(('rep', 'expert', 'data'))
- output 3: float32 [128, 512, 192], P(('rep', 'expert'), 'data')
- output 4: float32 [128, 512, 192], P(('rep', 'expert'), 'data')
- output 5: float32 [128, 192, 512], P(('rep', 'expert'), None, 'data')
All inputs are finite; a program needn't handle non-finite values.
Results may differ from a plain program's by a relative error of at most 0.001.
Values are sent between devices in bfloat16 or wider.
A program may use at most 1 GiB of HBM per device.

v0:
```python
import jax
import jax.numpy as jnp
from jax import lax
from jax.sharding import PartitionSpec as P


def route_plan(pair_ids, block_expert, block_of_expert, capacity):
    pair_count = pair_ids.shape[0]
    n_exp = block_expert.shape[0]
    pair_order = jnp.argsort(pair_ids, stable=True)
    sorted_ids = jnp.take(pair_ids, pair_order)
    all_exp = jnp.arange(n_exp, dtype=pair_ids.dtype)
    exp_start = jnp.searchsorted(sorted_ids, all_exp, side="left")
    exp_end = jnp.searchsorted(sorted_ids, all_exp, side="right")
    pair_rank = jnp.argsort(pair_order, stable=True)
    pair_slot = pair_rank - jnp.take(exp_start, pair_ids)
    pair_dest = jnp.where(pair_slot < capacity, jnp.take(block_of_expert, pair_ids) * capacity + pair_slot, n_exp * capacity)
    seat_ids = jnp.arange(capacity)
    seat_start = jnp.take(exp_start, block_expert)[:, None] + seat_ids[None, :]
    seat_count = jnp.take(exp_end - exp_start, block_expert)[:, None]
    src_pair = jnp.where(seat_ids[None, :] < seat_count, jnp.take(pair_order, jnp.minimum(seat_start, pair_count - 1)), pair_count)
    return src_pair.reshape(-1), pair_dest


def gather_rows(table, index):
    return jnp.take(table, index, axis=0, mode="fill", fill_value=0)


def solution(mesh):
    ep_size = mesh.shape["expert"]
    row_spec = P(("rep", "expert", "data"), None)
    wide_spec = P("expert", "data", None)
    down_spec = P("expert", None, "data")
    wide_out = P(("rep", "expert"), "data", None)
    down_out = P(("rep", "expert"), None, "data")

    def local_step(tok_in, expert_idx, gate_wt, w_gate, w_up, w_down, grad_out):
        tokens, top_k = expert_idx.shape
        width = tok_in.shape[1]
        n_loc = w_gate.shape[0]
        n_exp = n_loc * ep_size
        capacity = (5 * top_k * tokens + 4 * n_exp - 1) // (4 * n_exp)
        loc_ids = jnp.arange(n_loc, dtype=jnp.int32)
        pos_ids = jnp.arange(ep_size, dtype=jnp.int32)
        block_expert = (pos_ids[None, :] * n_loc + loc_ids[:, None]).reshape(-1)
        all_exp = jnp.arange(n_exp, dtype=jnp.int32)
        block_of_expert = (all_exp % n_loc) * ep_size + all_exp // n_loc
        src_pair, pair_dest = route_plan(expert_idx.reshape(-1), block_expert, block_of_expert, capacity)
        src_tok = src_pair // top_k
        buf_shape = (n_loc, ep_size, capacity, width)

        send_rows = gather_rows(tok_in, src_tok).reshape(buf_shape)
        recv_rows = lax.all_to_all(send_rows, "expert", 1, 1, tiled=True)
        wg_full = lax.all_gather(w_gate, "data", axis=1, tiled=True)
        wu_full = lax.all_gather(w_up, "data", axis=1, tiled=True)
        wd_full = lax.all_gather(w_down, "data", axis=2, tiled=True)
        pre_gate = jnp.einsum("lscd,ldf->lscf", recv_rows, wg_full, preferred_element_type=jnp.float32)
        pre_up = jnp.einsum("lscd,ldf->lscf", recv_rows, wu_full, preferred_element_type=jnp.float32)
        sig_gate = jax.nn.sigmoid(pre_gate)
        silu_gate = pre_gate * sig_gate
        hid_act = (silu_gate * pre_up).astype(jnp.bfloat16)
        exp_out = jnp.einsum("lscf,lfd->lscd", hid_act, wd_full, preferred_element_type=jnp.float32).astype(jnp.bfloat16)
        back_out = lax.all_to_all(exp_out, "expert", 1, 1, tiled=True).reshape(-1, width)
        pair_out = gather_rows(back_out, pair_dest).reshape(tokens, top_k, width)
        tok_out = (tok_in.astype(jnp.float32) + jnp.sum(gate_wt[:, :, None] * pair_out.astype(jnp.float32), axis=1)).astype(jnp.bfloat16)

        gate_rows = gather_rows(gate_wt.reshape(-1), src_pair)
        dy_rows = gather_rows(grad_out, src_tok)
        send_cots = (gate_rows[:, None] * dy_rows.astype(jnp.float32)).astype(jnp.bfloat16).reshape(buf_shape)
        recv_cots = lax.all_to_all(send_cots, "expert", 1, 1, tiled=True)
        part_down = jnp.einsum("lscf,lscd->lfd", hid_act, recv_cots, preferred_element_type=jnp.float32)
        grad_hid = jnp.einsum("lscd,lfd->lscf", recv_cots, wd_full, preferred_element_type=jnp.float32)
        grad_pre_gate = (grad_hid * pre_up * sig_gate * (1.0 + pre_gate * (1.0 - sig_gate))).astype(jnp.bfloat16)
        grad_pre_up = (grad_hid * silu_gate).astype(jnp.bfloat16)
        part_gate = jnp.einsum("lscd,lscf->ldf", recv_rows, grad_pre_gate, preferred_element_type=jnp.float32)
        part_up = jnp.einsum("lscd,lscf->ldf", recv_rows, grad_pre_up, preferred_element_type=jnp.float32)
        grad_rows = (jnp.einsum("lscf,ldf->lscd", grad_pre_gate, wg_full, preferred_element_type=jnp.float32) + jnp.einsum("lscf,ldf->lscd", grad_pre_up, wu_full, preferred_element_type=jnp.float32)).astype(jnp.bfloat16)
        back_grad = lax.all_to_all(grad_rows, "expert", 1, 1, tiled=True).reshape(-1, width)
        pair_grad = gather_rows(back_grad, pair_dest).reshape(tokens, top_k, width)
        grad_in = (grad_out.astype(jnp.float32) + jnp.sum(pair_grad.astype(jnp.float32), axis=1)).astype(jnp.bfloat16)
        grad_gate = lax.psum_scatter(part_gate, "data", scatter_dimension=1, tiled=True)
        grad_up = lax.psum_scatter(part_up, "data", scatter_dimension=1, tiled=True)
        grad_down = lax.psum_scatter(part_down, "data", scatter_dimension=2, tiled=True)
        return tok_out, grad_in, grad_gate, grad_up, grad_down

    return jax.shard_map(local_step, mesh=mesh, in_specs=(row_spec, row_spec, row_spec, wide_spec, wide_spec, down_spec, row_spec), out_specs=(row_spec, row_spec, wide_out, wide_out, down_out), check_vma=False)
```

profile of v0, /device:TPU:1, one launch (start us, length us, event | category | flops | bytes accessed | tf_op | source)
XLA Modules:
  0.0 1737.3 jit_solution(12665905798571095243)
XLA Ops:
  16.8 90.7 %gather_fusion.2 = s32[16384]{0:T(1024)S(1)} fusion(s32[16384]{0:T(1024)S(1)} %reshape.245, s32[16384]{0:T(1024)S(1)} %fusion.43), kind=kCustom, calls=%fused_computation.10 | custom fusion | bytes 196608 | tf_op jit(solution)/shard_map/jit(_take)/gather | solution.py:11
  107.6 18.3 %while.49 = (s32[]{:T(128)}, u32[128]{0:T(128)S(1)}, u32[128]{0:T(128)S(1)}, s32[16384]{0:T(1024)S(1)}, s32[]{:T(128)}, /*index=5*/s32[]{:T(128)}, s32[]{}) while((s32[]{:T(128)}, u32[128]{0:T(128)S(1)}, u32[128]{0:T(128)S(1)}, s32[16384]{0:T(1024)S(1)}, s32[]{:T(128)}, /*index=5*/s32[]{:T(128)}, s32[]{}) %tuple.75), condition=%wide.region_4.5_spmd.clone, body=%wide.region_3.4_spmd.clone.sunk | while | flops 2692 | bytes 10340 | solution.py:13
  125.8 18.3 %while.48 = (s32[]{:T(128)}, u32[128]{0:T(128)S(1)}, u32[128]{0:T(128)S(1)}, s32[16384]{0:T(1024)S(1)}, s32[]{:T(128)}, /*index=5*/s32[]{:T(128)}, s32[]{}) while((s32[]{:T(128)}, u32[128]{0:T(128)S(1)}, u32[128]{0:T(128)S(1)}, s32[16384]{0:T(1024)S(1)}, s32[]{:T(128)}, /*index=5*/s32[]{:T(128)}, s32[]{}) %tuple.93), condition=%wide.region_2.3_spmd.clone, body=%wide.region_1.2_spmd.clone.sunk | while | flops 2692 | bytes 10340 | solution.py:14
  148.9 113.0 %gather_fusion.3 = s32[20480]{0:T(1024)S(1)} fusion(s32[16384]{0:T(1024)S(1)} %get-tuple-element.141, s32[20480]{0:T(1024)S(1)} %broadcast_clamp_fusion.2), kind=kCustom, calls=%fused_computation.11 | custom fusion | bytes 245760 | tf_op jit(solution)/shard_map/jit(_take)/gather | solution.py:21
  262.3 113.0 %gather_fusion.4 = f32[20480]{0:T(1024)S(1)} fusion(f32[16384]{0:T(1024)S(1)} %reshape.248, s32[20480]{0:T(1024)S(1)} %broadcast_clamp_fusion.1), kind=kCustom, calls=%fused_computation.12 | custom fusion | bytes 245760 | tf_op jit(solution)/shard_map/jit(_take)/gather | solution.py:26
  375.6 82.8 %gather_fusion.7 = bf16[20480,512]{1,0:T(8,128)(2,1)} fusion(bf16[2048,512]{1,0:T(8,128)(2,1)S(1)} %copy-done.6, s32[20480]{0:T(1024)S(1)} %broadcast_clamp_fusion), kind=kCustom, calls=%fused_computation.3.clone | custom fusion | bytes 42024960 | tf_op jit(solution)/shard_map/jit(_take)/gather | solution.py:26
  484.2 82.9 %gather_fusion.11 = bf16[20480,512]{1,0:T(8,128)(2,1)} fusion(bf16[2048,512]{1,0:T(8,128)(2,1)S(1)} %copy-done.8, s32[20480]{0:T(1024)S(1)} %broadcast_clamp_fusion), kind=kCustom, calls=%fused_computation.7.clone | custom fusion | bytes 42024960 | tf_op jit(solution)/shard_map/jit(_take)/gather | solution.py:26
  567.0 15.9 multiply_convert_fusion
  583.0 17.7 %copy.24 = bf16[16,8,160,512]{3,2,0,1:T(8,128)(2,1)} copy(bf16[16,8,160,512]{3,2,1,0:T(8,128)(2,1)} %bitcast.60) | data formatting | bytes 41943040 | tf_op jit(solution)/shard_map/reshape | solution.py:69
  600.7 111.8 %all-to-all-done = bf16[16,8,160,512]{3,2,0,1:T(8,128)(2,1)} async-done(((bf16[16,8,160,512]{3,2,0,1:T(8,128)(2,1)}), bf16[16,8,160,512]{3,2,0,1:T(8,128)(2,1)}, u32[]{:S(2)}, u32[]{:S(2)}) %all-to-all-start) | async-done | bytes 20971552 | tf_op jit(solution)/shard_map/all_to_all | solution.py:53
  721.8 54.1 %all-gather.4.cloned.1.call-done = bf16[16,512,192]{2,1,0:T(8,128)(2,1)} async-done(((bf16[16,32,192]{2,1,0:T(8,128)(2,1)}), bf16[16,512,192]{2,1,0:T(8,128)(2,1)}) %all-gather.4.cloned.1.call-update) | async-done | bytes 3145744 | tf_op jit(solution)/shard_map/all_gather | solution.py:54
  775.9 15.3 fusion.16
  791.2 37.6 %all-gather.8.cloned.1.call-done = bf16[16,192,512]{1,2,0:T(8,128)(2,1)} async-done(((bf16[16,192,32]{1,2,0:T(8,128)(2,1)}), bf16[16,192,512]{1,2,0:T(8,128)(2,1)}) %all-gather.8.cloned.1.call-update) | async-done | bytes 3145744 | tf_op jit(solution)/shard_map/all_gather | solution.py:56
  828.8 119.1 %all-to-all-done.2 = bf16[16,8,160,512]{3,2,0,1:T(8,128)(2,1)} async-done(((bf16[16,8,160,512]{3,2,0,1:T(8,128)(2,1)}), bf16[16,8,160,512]{3,2,0,1:T(8,128)(2,1)}, u32[]{:S(2)}, u32[]{:S(2)}) %all-to-all-start.2) | async-done | bytes 20971552 | tf_op jit(solution)/shard_map/all_to_all | solution.py:70
  947.9 15.2 fusion.12
  963.2 32.3 %multiply_convert_fusion.3 = (bf16[16,8,160,192]{3,2,1,0:T(8,128)(2,1)}, bf16[16,8,160,192]{3,2,1,0:T(8,128)(2,1)}, bf16[16,8,160,192]{3,2,1,0:T(8,128)(2,1)}) fusion(f32[16,8,160,192]{3,2,1,0:T(8,128)} %fusion.16, f32[16,8,160,192]{3,2,1,0:T(8,128)} %fusion.12, bf16[16,512,192]{2,1,0:T(8,128)(2,1)} %all-gather.6.cloned.1.call-done, ...), kind=kOutput, calls=%fused_computation.36 | convolution fusion | flops 4085514240 | bytes 79167488 | tf_op jit(solution)/shard_map/lscd,ldf->lscf/dot_general | solution.py:58
  995.5 14.6 convolution_convert_fusion
  1010.1 17.7 %copy.21 = bf16[16,8,160,512]{3,2,0,1:T(8,128)(2,1)} copy(bf16[16,8,160,512]{3,2,1,0:T(8,128)(2,1)} %convolution_convert_fusion) | data formatting | bytes 41943040 | tf_op jit(solution)/shard_map/convert_element_type | solution.py:62
  1034.8 16.8 fusion.35
  1051.7 16.4 fusion.32
  1068.1 19.7 %fusion.24 = f32[16,8,160,512]{3,2,1,0:T(8,128)} fusion(bf16[16,8,160,192]{3,2,1,0:T(8,128)(2,1)} %get-tuple-element.206, bf16[16,512,192]{2,1,0:T(8,128)(2,1)} %all-gather.4.cloned.1.call-done), kind=kOutput, calls=%fused_computation.55 | convolution fusion | flops 4026531840 | bytes 52953088 | tf_op jit(solution)/shard_map/lscf,ldf->lscd/dot_general | solution.py:77
  1087.8 26.8 %add_convert_fusion = bf16[16,8,160,512]{3,2,1,0:T(8,128)(2,1)} fusion(f32[16,8,160,512]{3,2,1,0:T(8,128)} %fusion.24, bf16[16,8,160,192]{3,2,1,0:T(8,128)(2,1)} %get-tuple-element.207, bf16[16,512,192]{2,1,0:T(8,128)(2,1)} %all-gather.6.cloned.1.call-done), kind=kOutput, calls=%fused_computation.29 | convolution fusion | flops 4047503360 | bytes 73924608 | tf_op jit(solution)/shard_map/lscf,ldf->lscd/dot_general | solution.py:77
  1114.6 17.7 %copy.26 = bf16[16,8,160,512]{3,2,0,1:T(8,128)(2,1)} copy(bf16[16,8,160,512]{3,2,1,0:T(8,128)(2,1)} %add_convert_fusion) | data formatting | bytes 41943040 | tf_op jit(solution)/shard_map/convert_element_type | solution.py:77
  1132.3 130.9 %all-to-all-done.1 = bf16[16,8,160,512]{3,2,0,1:T(8,128)(2,1)} async-done(((bf16[16,8,160,512]{3,2,0,1:T(8,128)(2,1)}), bf16[16,8,160,512]{3,2,0,1:T(8,128)(2,1)}, u32[]{:S(2)}, u32[]{:S(2)}) %all-to-all-start.1) | async-done | bytes 20971552 | tf_op jit(solution)/shard_map/all_to_all | solution.py:63
  1270.3 16.7 fusion.29
  1287.0 97.2 %gather_fusion.8 = s32[16384]{0:T(1024)S(1)} fusion(s32[128]{0:T(128)S(1)} %copy-done.1, s32[16384]{0:T(1024)S(1)} %fusion.44), kind=kCustom, calls=%fused_computation.4.clone | custom fusion | bytes 196608 | tf_op jit(solution)/shard_map/jit(_take)/gather | solution.py:16
  1384.2 97.2 %gather_fusion.9 = s32[16384]{0:T(1024)S(1)} fusion(s32[128]{0:T(128)S(1)} %fusion.46, s32[16384]{0:T(1024)S(1)} %fusion.44), kind=kCustom, calls=%fused_computation.8.clone | custom fusion | bytes 196608 | tf_op jit(solution)/shard_map/jit(_take)/gather | solution.py:17
  1489.3 17.9 %copy.22 = bf16[16,8,160,512]{3,2,1,0:T(8,128)(2,1)} copy(bf16[16,8,160,512]{3,2,0,1:T(8,128)(2,1)} %all-to-all-done.1) | data formatting | bytes 41943040 | tf_op jit(solution)/shard_map/all_to_all | solution.py:63
  1507.3 76.5 %gather_fusion.10 = bf16[16384,512]{1,0:T(8,128)(2,1)} fusion(bf16[20480,512]{1,0:T(8,128)(2,1)} %bitcast.59, s32[16384]{0:T(1024)S(1)} %broadcast_clamp_fusion.3), kind=kCustom, calls=%fused_computation.5.clone | custom fusion | bytes 33619968 | tf_op jit(solution)/shard_map/jit(_take)/gather | solution.py:26
  1583.8 17.7 %copy.27 = bf16[16,8,160,512]{3,2,1,0:T(8,128)(2,1)} copy(bf16[16,8,160,512]{3,2,0,1:T(8,128)(2,1)} %all-to-all-done.3) | data formatting | bytes 41943040 | tf_op jit(solution)/shard_map/all_to_all | solution.py:78
  1601.5 76.6 %gather_fusion.12 = bf16[16384,512]{1,0:T(8,128)(2,1)} fusion(bf16[20480,512]{1,0:T(8,128)(2,1)} %bitcast.58, s32[16384]{0:T(1024)S(1)} %broadcast_clamp_fusion.3), kind=kCustom, calls=%fused_computation.9.clone | custom fusion | bytes 33619968 | tf_op jit(solution)/shard_map/jit(_take)/gather | solution.py:26
  1678.1 46.2 %convert_reduce_fusion = (f32[2048,512]{1,0:T(8,128)S(1)}, f32[2048,512]{1,0:T(8,128)}) fusion(bf16[16384,512]{1,0:T(8,128)(2,1)} %gather_fusion.12, pred[16384]{0:T(1024)(128)(4,1)S(1)} %get-tuple-element.197, bf16[16384,512]{1,0:T(8,128)(2,1)} %gather_fusion.10, f32[2048,8]{1,0:T(8,128)S(1)} %copy-done.11), kind=kLoop, calls=%fused_computation.31 | loop fusion | flops 56623104 | bytes 42024960 | tf_op jit(solution)/shard_map/reduce_sum | solution.py:80
  (216 shorter events, 113.0 us)
Async XLA Ops:
  9.0 98.5 %copy-start.4 = (s32[16384]{0:T(1024)}, s32[16384]{0:T(1024)S(1)}, u32[]{:S(2)}) copy-start(s32[16384]{0:T(1024)S(1)} %reshape.245) | copy-start | bytes 196612
  16.8 132.1 %copy-start.2 = (s32[16384]{0:T(1024)}, s32[16384]{0:T(1024)S(1)}, u32[]{:S(2)}) copy-start(s32[16384]{0:T(1024)S(1)} %get-tuple-element.141) | copy-start | bytes 196612
  16.8 131.0 %copy-start.12 = (f32[2048,8]{0,1:T(8,128)S(1)}, f32[2048,8]{0,1:T(8,128)}, u32[]{:S(2)}) copy-start(f32[2048,8]{0,1:T(8,128)} %param.21) | copy-start | bytes 196612
  144.1 117.8 %copy-start = (s32[128]{0:T(128)}, s32[128]{0:T(128)S(1)}, u32[]{:S(2)}) copy-start(s32[128]{0:T(128)S(1)} %convert_element_type.66) | copy-start | bytes 1540
  148.2 113.7 %copy-start.10 = (f32[2048,8]{1,0:T(8,128)}, f32[2048,8]{1,0:T(8,128)S(1)}, u32[]{:S(2)}) copy-start(f32[2048,8]{1,0:T(8,128)S(1)} %copy.16) | copy-start | bytes 196612
  262.3 113.3 %copy-start.6 = (bf16[2048,512]{1,0:T(8,128)(2,1)S(1)}, bf16[2048,512]{1,0:T(8,128)(2,1)}, u32[]{:S(2)}) copy-start(bf16[2048,512]{1,0:T(8,128)(2,1)} %param.19) | copy-start | bytes 6291460
  476.7 7.5 copy-start.8
  476.7 235.8 %all-to-all-start = ((bf16[16,8,160,512]{3,2,0,1:T(8,128)(2,1)}), bf16[16,8,160,512]{3,2,0,1:T(8,128)(2,1)}, u32[]{:S(2)}, u32[]{:S(2)}) async-start(bf16[16,8,160,512]{3,2,0,1:T(8,128)(2,1)} %copy.18), calls=%async_computation | async-start | bytes 41943040 | tf_op jit(solution)/shard_map/all_to_all | solution.py:53
  712.5 235.4 %all-to-all-start.2 = ((bf16[16,8,160,512]{3,2,0,1:T(8,128)(2,1)}), bf16[16,8,160,512]{3,2,0,1:T(8,128)(2,1)}, u32[]{:S(2)}, u32[]{:S(2)}) async-start(bf16[16,8,160,512]{3,2,0,1:T(8,128)(2,1)} %copy.24), calls=%async_computation.2 | async-start | bytes 41943040 | tf_op jit(solution)/shard_map/all_to_all | solution.py:70
  719.6 56.3 %all-gather.4.cloned.1.call-start = ((), (), s32[]{:S(2)}) async-start(), calls=%async_computation.7 | async-start | bytes 4456448 | tf_op jit(solution)/shard_map/all_gather | solution.py:54
  720.3 108.5 %all-gather.8.cloned.1.call-start = ((), (), s32[]{:S(2)}) async-start(), calls=%async_computation.9 | async-start | bytes 4456448 | tf_op jit(solution)/shard_map/all_gather | solution.py:56
  721.0 242.1 %all-gather.6.cloned.1.call-start = ((), (), s32[]{:S(2)}) async-start(), calls=%async_computation.8 | async-start | bytes 4456448 | tf_op jit(solution)/shard_map/all_gather | solution.py:55
  1027.7 235.4 %all-to-all-start.1 = ((bf16[16,8,160,512]{3,2,0,1:T(8,128)(2,1)}), bf16[16,8,160,512]{3,2,0,1:T(8,128)(2,1)}, u32[]{:S(2)}, u32[]{:S(2)}) async-start(bf16[16,8,160,512]{3,2,0,1:T(8,128)(2,1)} %copy.21), calls=%async_computation.1 | async-start | bytes 41943040 | tf_op jit(solution)/shard_map/all_to_all | solution.py:63
  1034.8 695.4 %reduce-scatter.8.cloned.1.call-start = ((), (), s32[]{:S(2)}) async-start(), calls=%async_computation.12 | async-start | bytes 8912896 | tf_op jit(solution)/shard_map/reduce_scatter | solution.py:83
  1051.6 678.6 %reduce-scatter.6.cloned.1.call-start = ((), (), s32[]{:S(2)}) async-start(), calls=%async_computation.11 | async-start | bytes 8912896 | tf_op jit(solution)/shard_map/reduce_scatter | solution.py:82
  1263.2 320.6 %all-to-all-start.3 = ((bf16[16,8,160,512]{3,2,0,1:T(8,128)(2,1)}), bf16[16,8,160,512]{3,2,0,1:T(8,128)(2,1)}, u32[]{:S(2)}, u32[]{:S(2)}) async-start(bf16[16,8,160,512]{3,2,0,1:T(8,128)(2,1)} %copy.26), calls=%async_computation.3 | async-start | bytes 41943040 | tf_op jit(solution)/shard_map/all_to_all | solution.py:78
  1270.2 16.7 copy-start.5
  1270.2 16.8 copy-start.1
  1270.2 460.0 %reduce-scatter.4.cloned.1.call-start = ((), (), s32[]{:S(2)}) async-start(), calls=%async_computation.10 | async-start | bytes 8912896 | tf_op jit(solution)/shard_map/reduce_scatter | solution.py:81
  1384.2 97.2 %copy-start.3 = (s32[16384]{0:T(1024)S(1)}, s32[16384]{0:T(1024)}, u32[]{:S(2)}) copy-start(s32[16384]{0:T(1024)} %copy-done.2) | copy-start | bytes 196612
  1601.5 76.7 %copy-start.11 = (f32[2048,8]{1,0:T(8,128)S(1)}, f32[2048,8]{1,0:T(8,128)}, u32[]{:S(2)}) copy-start(f32[2048,8]{1,0:T(8,128)} %copy-done.10) | copy-start | bytes 196612
  1678.1 46.2 %copy-start.7 = (bf16[2048,512]{1,0:T(8,128)(2,1)S(1)}, bf16[2048,512]{1,0:T(8,128)(2,1)}, u32[]{:S(2)}) copy-start(bf16[2048,512]{1,0:T(8,128)(2,1)} %param.19) | copy-start | bytes 6291460
  1678.1 46.2 %copy-start.9 = (bf16[2048,512]{1,0:T(8,128)(2,1)S(1)}, bf16[2048,512]{1,0:T(8,128)(2,1)}, u32[]{:S(2)}) copy-start(bf16[2048,512]{1,0:T(8,128)(2,1)} %param.25) | copy-start | bytes 6291460
Sparse Core Ops, SparseCore 0:
  722.5 53.3 all-gather.3
  778.0 50.7 all-gather.7
  831.0 50.7 all-gather.5
  1051.8 86.6 reduce-scatter.7
  1142.3 84.7 reduce-scatter.5
  1287.1 86.3 reduce-scatter.3
where the time goes:
time: 1740 us
  local copies, waits for them, and re-layouts  967 us (56%)
  waiting for transfers between devices  456 us (26%)
  matrix products  174 us (10%)
  other arithmetic  96.2 us (6%)
  starting transfers between devices  28.8 us (2%)
    gather x5, local copies, waits for them, and re-layouts, gather_rows(): return jnp.take(table, index, axis=0, mode='fill', fill_value=0)  432 us
    all_to_all x1, waiting for transfers between devices, local_step(): lax.all_to_all(exp_out, 'expert', 1, 1, tiled=True).reshape(-1, width)  131 us
    all_to_all x1, waiting for transfers between devices, local_step(): recv_cots = lax.all_to_all(send_cots, 'expert', 1, 1, tiled=True)  119 us
    gather x1, local copies, waits for them, and re-layouts, route_plan(): jnp.take(pair_order, jnp.minimum(seat_start, pair_count - 1))  113 us
    all_to_all x1, waiting for transfers between devices, local_step(): recv_rows = lax.all_to_all(send_rows, 'expert', 1, 1, tiled=True)  112 us
    gather x1, local copies, waits for them, and re-layouts, route_plan(): pair_slot = pair_rank - jnp.take(exp_start, pair_ids)  97.2 us
    gather x1, local copies, waits for them, and re-layouts, route_plan(): jnp.take(block_of_expert, pair_ids) * capacity + pair_slot  97.2 us
    gather x1, local copies, waits for them, and re-layouts, route_plan(): sorted_ids = jnp.take(pair_ids, pair_order)  90.7 us
  transfers between devices with their start and end apart: 10, of which 5 were waited for; matrix products, arithmetic and copies ran while one was open for 41% of the time, Pallas kernels for 0%

commit v1 on v0

v1 whole, which is shorter than its diff:
```python
import functools

import jax
import jax.numpy as jnp
from jax import lax
from jax.experimental import pallas as pl
from jax.experimental.pallas import tpu as pltpu
from jax.sharding import PartitionSpec as P


LANES = 128
GROUP = 3072
VMEM_BIG = 60 * 1024 * 1024


def ceil_to(n, m):
    return (n + m - 1) // m * m


def call(body, interpret=False, **kw):
    return pl.pallas_call(body, **kw)


def route_body(cap, stride, n_loc, ids_ref, dest_ref):
    top_k, tokens = ids_ref.shape
    n_exp = 128
    blk = min(256, tokens)
    before = (lax.broadcasted_iota(jnp.int32, (blk, blk), 0) < lax.broadcasted_iota(jnp.int32, (blk, blk), 1)).astype(jnp.bfloat16)
    exp_iota = lax.broadcasted_iota(jnp.int32, (n_exp, blk), 0)
    n_pos = n_exp // n_loc
    base = jnp.zeros((n_exp, 1), jnp.float32)
    for b in range(tokens // blk):
        ids = ids_ref[:, b * blk : (b + 1) * blk]
        hits = [exp_iota == ids[j : j + 1, :] for j in range(top_k)]
        any_hit = functools.reduce(jnp.logical_or, hits)
        hot = jnp.where(any_hit, 1.0, 0.0)
        rank = jnp.dot(hot.astype(jnp.bfloat16), before, preferred_element_type=jnp.float32) + base
        base = base + jnp.sum(hot, axis=1, keepdims=True)
        rows = []
        for j in range(top_k):
            slot = jnp.sum(jnp.where(hits[j], rank, 0.0), axis=0, keepdims=True).astype(jnp.int32)
            e = ids[j : j + 1, :]
            rows.append(jnp.where(slot < cap, (e // n_loc) * GROUP + (e % n_loc) * stride + slot, n_pos * GROUP))
        dest_ref[:, b * blk : (b + 1) * blk] = jnp.concatenate(rows, axis=0)


def list_body(top_k, tokens, fill_ref, dest_ref, list_ref, sem):
    copy = pltpu.make_async_copy(fill_ref, list_ref, sem)
    copy.start()
    copy.wait()
    unroll = 4

    def step(i, carry):
        for u in range(unroll):
            t = i * unroll + u
            for j in range(top_k):
                list_ref[dest_ref[j * tokens + t]] = t * top_k + j
        return carry

    lax.fori_loop(0, tokens // unroll, step, 0)


def make_list(expert_idx, cap, stride, n_loc):
    tokens, top_k = expert_idx.shape
    n_pos = 128 // n_loc
    dest = pl.pallas_call(
        functools.partial(route_body, cap, stride, n_loc),
        out_shape=jax.ShapeDtypeStruct((top_k, tokens), jnp.int32),
        in_specs=[pl.BlockSpec(memory_space=pltpu.VMEM)],
        out_specs=pl.BlockSpec(memory_space=pltpu.VMEM),
        cost_estimate=pl.CostEstimate(flops=4_000_000_000, bytes_accessed=1 << 17, transcendentals=0),
        name="route",
    )(expert_idx.T)
    size = n_pos * GROUP + 1024
    fill = jnp.full((size,), tokens * top_k, jnp.int32)
    return pl.pallas_call(
        functools.partial(list_body, top_k, tokens),
        out_shape=jax.ShapeDtypeStruct((size,), jnp.int32),
        in_specs=[pl.BlockSpec(memory_space=pl.ANY), pl.BlockSpec(memory_space=pltpu.SMEM)],
        out_specs=pl.BlockSpec(memory_space=pltpu.SMEM),
        scratch_shapes=[pltpu.SemaphoreType.DMA],
        cost_estimate=pl.CostEstimate(flops=10_000_000_000, bytes_accessed=1 << 17, transcendentals=0),
        name="lists",
    )(fill, dest.reshape(-1))


def load_lists(groups_ref, list_ref, gate_ref, lists, gates, sems):
    copies = [pltpu.make_async_copy(list_ref.at[pl.ds(pl.multiple_of(groups_ref[g] * GROUP, GROUP), GROUP)], lists.at[pl.ds(g * GROUP, GROUP)], sems.at[g]) for g in range(2)]
    copies.append(pltpu.make_async_copy(gate_ref, gates, sems.at[2]))
    for c in copies:
        c.start()
    for c in copies:
        c.wait()


def dispatch_body(n_blk, stride, top_k, n_loc, groups_ref, list_ref, gate_ref, x_ref, dy_ref, r_ref, c_ref, lists, gates, rows, tile, sems):
    i = pl.program_id(0)
    tokens, width = x_ref.shape
    parts = width // LANES
    slab = 2 * parts
    span = stride + 1

    @pl.when(i == 0)
    def _():
        load_lists(groups_ref, list_ref, gate_ref, lists, gates, sems)
        rows[pl.ds(tokens * slab, slab), :] = jnp.zeros((slab, LANES), jnp.float32)

        def fill(b, carry):
            t0 = pl.multiple_of(b * 16, 16)
            xs = x_ref[pl.ds(t0, 16), :].astype(jnp.float32)
            ds = dy_ref[pl.ds(t0, 16), :].astype(jnp.float32)
            for k in range(parts):
                rows[pl.ds(t0 * slab + k, 16, stride=slab), :] = xs[:, k * LANES : (k + 1) * LANES]
                rows[pl.ds(t0 * slab + parts + k, 16, stride=slab), :] = ds[:, k * LANES : (k + 1) * LANES]
            return carry

        lax.fori_loop(0, tokens // 16, fill, 0)

    upper = lax.broadcasted_iota(jnp.int32, (slab, LANES), 0) < parts
    for b in range(n_blk):
        e = i * n_blk + b
        base = (e // n_loc) * GROUP + (e % n_loc) * stride

        def gather(q, carry, base=base):
            for u in range(16):
                s = q * 16 + u
                p = lists[base + s]
                row = rows[pl.ds(pl.multiple_of((p // top_k) * slab, slab), slab), :]
                tile[pl.ds(s, slab, stride=span), :] = row * jnp.where(upper, 1.0, gates[p])
            return carry

        lax.fori_loop(0, stride // 16, gather, 0)
        for k in range(parts):
            r_ref[b, :, k * LANES : (k + 1) * LANES] = tile[pl.ds(k * span, stride), :].astype(jnp.bfloat16)
            c_ref[b, :, k * LANES : (k + 1) * LANES] = tile[pl.ds((parts + k) * span, stride), :].astype(jnp.bfloat16)


def dispatch(groups, lists, gates, x, dy, stride, top_k, n_loc, n_blk=4):
    tokens, width = x.shape
    slab = 2 * (width // LANES)
    n_mine = 2 * n_loc
    shape = jax.ShapeDtypeStruct((n_mine, stride, width), jnp.bfloat16)
    spec = pl.BlockSpec((n_blk, stride, width), lambda i: (i, 0, 0))
    return pl.pallas_call(
        functools.partial(dispatch_body, n_blk, stride, top_k, n_loc),
        grid=(n_mine // n_blk,),
        out_shape=(shape, shape),
        in_specs=[
            pl.BlockSpec(memory_space=pltpu.SMEM),
            pl.BlockSpec(memory_space=pl.ANY),
            pl.BlockSpec(memory_space=pl.ANY),
            pl.BlockSpec(memory_space=pltpu.VMEM),
            pl.BlockSpec(memory_space=pltpu.VMEM),
        ],
        out_specs=(spec, spec),
        scratch_shapes=[
            pltpu.SMEM((2 * GROUP,), jnp.int32),
            pltpu.SMEM(gates.shape, jnp.float32),
            pltpu.VMEM(((tokens + 1) * slab, LANES), jnp.float32),
            pltpu.VMEM((ceil_to(slab * (stride + 1), 8), LANES), jnp.float32),
            pltpu.SemaphoreType.DMA((3,)),
        ],
        compiler_params=pltpu.CompilerParams(dimension_semantics=("arbitrary",), vmem_limit_bytes=VMEM_BIG),
        cost_estimate=pl.CostEstimate(flops=10_000_000_000, bytes_accessed=1 << 24, transcendentals=0),
        name="dispatch",
    )(groups, lists, gates, x, dy)


def combine_body(n_blk, stride, top_k, n_loc, groups_ref, list_ref, gate_ref, o_ref, dr_ref, out_ref, lists, gates, acc, tile, sems):
    i = pl.program_id(0)
    tokens = out_ref.shape[0]
    width = o_ref.shape[-1]
    parts = width // LANES
    slab = 2 * parts
    span = stride + 1

    @pl.when(i == 0)
    def _():
        load_lists(groups_ref, list_ref, gate_ref, lists, gates, sems)

        def clear(b, carry):
            acc[pl.ds(pl.multiple_of(b * 8 * slab, 8 * slab), 8 * slab), :] = jnp.zeros((8 * slab, LANES), jnp.float32)
            return carry

        lax.fori_loop(0, tokens // 8, clear, 0)

    upper = lax.broadcasted_iota(jnp.int32, (slab, LANES), 0) < parts
    for b in range(n_blk):
        e = i * n_blk + b
        base = (e // n_loc) * GROUP + (e % n_loc) * stride
        for k in range(parts):
            tile[pl.ds(k * span, stride), :] = o_ref[0, b, :, k * LANES : (k + 1) * LANES].astype(jnp.float32)
            tile[pl.ds((parts + k) * span, stride), :] = dr_ref[0, b, :, k * LANES : (k + 1) * LANES].astype(jnp.float32)

        def scatter(q, carry, base=base):
            for half in range(2):
                at, sums = [], []
                for u in range(8):
                    s = q * 16 + half * 8 + u
                    p = lists[base + s]
                    a = pl.multiple_of((p // top_k) * slab, slab)
                    row = tile[pl.ds(s, slab, stride=span), :] * jnp.where(upper, gates[p], 1.0)
                    at.append(a)
                    sums.append(acc[pl.ds(a, slab), :] + row)
                for a, v in zip(at, sums):
                    acc[pl.ds(a, slab), :] = v
            return carry

        lax.fori_loop(0, stride // 16, scatter, 0)

    @pl.when(i == pl.num_programs(0) - 1)
    def _():
        def write(b, carry):
            t0 = pl.multiple_of(b * 8, 8)
            for k in range(slab):
                out_ref[pl.ds(t0, 8), k * LANES : (k + 1) * LANES] = acc[pl.ds(t0 * slab + k, 8, stride=slab), :]
            return carry

        lax.fori_loop(0, tokens // 8, write, 0)


def combine(block, groups, lists, gates, o, dr, tokens, stride, top_k, n_loc, n_blk=4):
    width = o.shape[-1]
    slab = 2 * (width // LANES)
    n_mine = 2 * n_loc
    spec = pl.BlockSpec((1, n_blk, stride, width), lambda i: (block, i, 0, 0))
    return pl.pallas_call(
        functools.partial(combine_body, n_blk, stride, top_k, n_loc),
        grid=(n_mine // n_blk,),
        out_shape=jax.ShapeDtypeStruct((tokens, 2 * width), jnp.float32),
        in_specs=[
            pl.BlockSpec(memory_space=pltpu.SMEM),
            pl.BlockSpec(memory_space=pl.ANY),
            pl.BlockSpec(memory_space=pl.ANY),
            spec,
            spec,
        ],
        out_specs=pl.BlockSpec(memory_space=pltpu.VMEM),
        scratch_shapes=[
            pltpu.SMEM((2 * GROUP,), jnp.int32),
            pltpu.SMEM(gates.shape, jnp.float32),
            pltpu.VMEM(((tokens + 1) * slab, LANES), jnp.float32),
            pltpu.VMEM((ceil_to(slab * (stride + 1), 8), LANES), jnp.float32),
            pltpu.SemaphoreType.DMA((3,)),
        ],
        compiler_params=pltpu.CompilerParams(dimension_semantics=("arbitrary",), vmem_limit_bytes=VMEM_BIG),
        cost_estimate=pl.CostEstimate(flops=14_000_000_000, bytes_accessed=1 << 24, transcendentals=0),
        name="combine",
    )(groups, lists, gates, o, dr)


def pack_body(g_ref, u_ref, d_ref, out_ref):
    n, rows, _ = g_ref.shape
    half = rows // 2
    low = lax.broadcasted_iota(jnp.int32, (half, LANES), 1) < LANES // 2
    for e in range(n):
        for m, ref in enumerate((g_ref, u_ref, d_ref)):
            base = m * (rows + half)
            out_ref[e, base : base + rows, :] = ref[e, :, :LANES]
            rest = jnp.concatenate([ref[e, :, LANES:], jnp.zeros((rows, LANES // 2), ref.dtype)], axis=1).astype(jnp.float32)
            both = jnp.where(low, rest[:half], pltpu.roll(rest[half:], LANES // 2, 1))
            out_ref[e, base + rows : base + rows + half, :] = both.astype(out_ref.dtype)


def pack_weights(w_gate, w_up, w_down_t):
    n, rows, _ = w_gate.shape
    return pl.pallas_call(
        pack_body,
        out_shape=jax.ShapeDtypeStruct((n, 3 * (rows + rows // 2), LANES), w_gate.dtype),
        cost_estimate=pl.CostEstimate(flops=1_000_000_000, bytes_accessed=1 << 21, transcendentals=0),
        name="pack",
    )(w_gate, w_up, w_down_t)


def unpack_body(half_n, n_in, *refs):
    ins, outs = refs[: 2 * n_in], refs[2 * n_in :]
    rows = outs[0].shape[1]
    half = rows // 2
    at = 0
    for k in range(n_in):
        mine, theirs = ins[2 * k], ins[2 * k + 1]
        for e in range(half_n):
            for m, out in enumerate(outs):
                base = m * (rows + half)
                out[at, :, :LANES] = mine[e, base : base + rows, :] + theirs[e, base : base + rows, :]
                rest = mine[e, base + rows : base + rows + half, :] + theirs[e, base + rows : base + rows + half, :]
                out[at, :half, LANES:] = rest[:, : LANES // 2]
                out[at, half:, LANES:] = pltpu.roll(rest, LANES // 2, 1)[:, : LANES // 2]
            at += 1


def unpack_grads(pairs, n_loc, rows, f_dim):
    half_n = pairs[0][1].shape[0]
    shape = jax.ShapeDtypeStruct((n_loc, rows, f_dim), jnp.float32)
    flat = [a for p in pairs for a in p]
    return pl.pallas_call(
        functools.partial(unpack_body, half_n, len(pairs)),
        out_shape=(shape,) * 3,
        cost_estimate=pl.CostEstimate(flops=1_000_000_000, bytes_accessed=1 << 22, transcendentals=0),
        compiler_params=pltpu.CompilerParams(vmem_limit_bytes=VMEM_BIG),
        name="unpack",
    )(*flat)


def shard_index(z, y, first, a, b, sign):
    dz, dy = (a, b) if first == "z" else (b, a)
    return lax.rem(z + sign * dz + 4, 4) * 4 + lax.rem(y + sign * dy + 4, 4)


def experts_body(n_sets, last, first, has_prev, *refs):
    place = refs[0]
    r_refs = refs[1 : 1 + n_sets]
    c_refs = refs[1 + n_sets : 1 + 2 * n_sets]
    at = 1 + 2 * n_sets
    w_refs = refs[at : at + 5]
    at += 5 + (2 if has_prev else 0)
    o_ref, dr_ref = refs[at : at + 2]
    g_refs = refs[at + 2 : at + 7]
    wgu, wd, ab, dh, hid, dab, dwgu, dwd = refs[at + 7 :]
    z, y = place[0], place[1]
    stride, width = r_refs[0].shape[1:]
    rows = width // 16
    half = rows // 2
    packed = rows + half
    f_pad = wd.shape[1]
    low = lax.broadcasted_iota(jnp.int32, (half, LANES), 1) < LANES // 2

    for a in range(4):
        for b in range(4):
            if a == 2:
                ref, slot = (w_refs[3], b) if b < 2 else (w_refs[4], b - 2)
            else:
                ref, slot = w_refs[(0, 1, None, 2)[a]], b
            k = shard_index(z, y, last, a, b, -1)
            row0 = pl.multiple_of(k * rows, rows)
            for m in range(3):
                base = m * packed
                dst, col = (wgu, m * f_pad) if m < 2 else (wd, 0)
                dst[pl.ds(row0, rows), col : col + LANES] = ref[slot, 0, base : base + rows, :]
                rest = ref[slot, 0, base + rows : base + packed, :].astype(jnp.float32)
                top = jnp.where(low, rest, 0.0)
                bottom = jnp.where(low, pltpu.roll(rest, LANES // 2, 1), 0.0)
                dst[pl.ds(row0, rows), col + LANES : col + 2 * LANES] = jnp.concatenate([top, bottom], axis=0).astype(dst.dtype)

    rows_all = jnp.concatenate([r[0] for r in r_refs], axis=0)
    cots_all = jnp.concatenate([c[0] for c in c_refs], axis=0)
    ab[...] = jnp.dot(rows_all, wgu[...], preferred_element_type=jnp.float32)
    dh[...] = jnp.dot(cots_all, wd[...], preferred_element_type=jnp.float32)

    def act(q, carry):
        r0 = pl.multiple_of(q * 32, 32)
        pre = ab[pl.ds(r0, 32), :f_pad]
        up = ab[pl.ds(r0, 32), f_pad:]
        grad = dh[pl.ds(r0, 32), :]
        sig = jax.nn.sigmoid(pre)
        silu = pre * sig
        hid[pl.ds(r0, 32), :] = (silu * up).astype(jnp.bfloat16)
        dab[pl.ds(r0, 32), :f_pad] = (grad * up * sig * (1.0 + pre * (1.0 - sig))).astype(jnp.bfloat16)
        dab[pl.ds(r0, 32), f_pad:] = (grad * silu).astype(jnp.bfloat16)
        return carry

    lax.fori_loop(0, n_sets * stride // 32, act, 0)

    nt = (((1,), (1,)), ((), ()))
    tn = (((0,), (0,)), ((), ()))
    out = lax.dot_general(hid[...], wd[...], nt, preferred_element_type=jnp.float32).astype(jnp.bfloat16)
    for s in range(n_sets):
        o_ref[s, 0] = out[s * stride : (s + 1) * stride]
    back = lax.dot_general(dab[...], wgu[...], nt, preferred_element_type=jnp.float32).astype(jnp.bfloat16)
    for s in range(n_sets):
        dr_ref[s, 0] = back[s * stride : (s + 1) * stride]
    dwgu[...] = lax.dot_general(rows_all, dab[...], tn, preferred_element_type=jnp.float32)
    dwd[...] = lax.dot_general(cots_all, hid[...], tn, preferred_element_type=jnp.float32)

    for a in range(4):
        for b in range(4):
            if a == 2:
                ref, slot = (g_refs[3], b) if b < 2 else (g_refs[4], b - 2)
            else:
                ref, slot = g_refs[(0, 1, None, 2)[a]], b
            k = shard_index(z, y, first, a, b, 1)
            row0 = pl.multiple_of(k * rows, rows)
            for m in range(3):
                base = m * packed
                src, col = (dwgu, m * f_pad) if m < 2 else (dwd, 0)
                ref[slot, 0, base : base + rows, :] = src[pl.ds(row0, rows), col : col + LANES]
                rest = src[pl.ds(row0, rows), col + LANES : col + 2 * LANES]
                ref[slot, 0, base + rows : base + packed, :] = jnp.where(low, rest[:half], pltpu.roll(rest[half:], LANES // 2, 1))


def experts(place, r_sets, c_sets, w_arrays, prev, colour, start, count, n_loc):
    n_sets = len(r_sets)
    n_mine, stride, width = r_sets[0].shape
    half_n = n_loc // 2
    packed = w_arrays[0].shape[2]
    off = colour * half_n + start
    first, last = ("y", "z") if colour == 0 else ("z", "y")
    total = 2 * count

    def mine(i):
        return jnp.where(i < count, off + i, n_loc + off + i - count)

    def held(i):
        return jnp.where(i < count, start + i, half_n + start + i - count)

    tok_spec = pl.BlockSpec((1, stride, width), lambda i: (mine(i), 0, 0))
    out_spec = pl.BlockSpec((n_sets, 1, stride, width), lambda i: (0, mine(i), 0, 0))
    out_shape = jax.ShapeDtypeStruct((n_sets, n_mine, stride, width), jnp.bfloat16)
    f_pad = 2 * LANES
    m_rows = n_sets * stride
    w_specs = [pl.BlockSpec((w.shape[0], 1, packed, LANES), lambda i: (0, held(i), 0, 0)) for w in w_arrays]
    g_slots = (4, 4, 4, 2, 2)
    g_specs = [pl.BlockSpec((n, 1, packed, LANES), lambda i: (0, i, 0, 0)) for n in g_slots]
    g_shapes = [jax.ShapeDtypeStruct((n, total, packed, LANES), jnp.float32) for n in g_slots]
    in_specs = [pl.BlockSpec(memory_space=pltpu.SMEM)] + [tok_spec] * (2 * n_sets) + w_specs
    args = [place, *r_sets, *c_sets, *w_arrays]
    aliases = {}
    if prev is not None:
        aliases = {len(args): 0, len(args) + 1: 1}
        in_specs += [pl.BlockSpec(memory_space=pl.ANY)] * 2
        args += list(prev)
    res = pl.pallas_call(
        functools.partial(experts_body, n_sets, last, first, prev is not None),
        grid=(total,),
        out_shape=[out_shape, out_shape] + g_shapes,
        in_specs=in_specs,
        out_specs=[out_spec, out_spec] + g_specs,
        scratch_shapes=[
            pltpu.VMEM((width, 2 * f_pad), jnp.bfloat16),
            pltpu.VMEM((width, f_pad), jnp.bfloat16),
            pltpu.VMEM((m_rows, 2 * f_pad), jnp.float32),
            pltpu.VMEM((m_rows, f_pad), jnp.float32),
            pltpu.VMEM((m_rows, f_pad), jnp.bfloat16),
            pltpu.VMEM((m_rows, 2 * f_pad), jnp.bfloat16),
            pltpu.VMEM((width, 2 * f_pad), jnp.float32),
            pltpu.VMEM((width, f_pad), jnp.float32),
        ],
        input_output_aliases=aliases,
        compiler_params=pltpu.CompilerParams(dimension_semantics=("arbitrary",), vmem_limit_bytes=VMEM_BIG),
        cost_estimate=pl.CostEstimate(flops=3_000_000_000 * total, bytes_accessed=6_000_000 * total, transcendentals=0),
        name="experts",
    )(*args)
    return (res[0], res[1]), res[2:]


def solution(mesh):
    n_pos = mesh.shape["expert"]
    chips_x = n_pos // 2
    row_spec = P(("rep", "expert", "data"), None)
    wide_spec = P("expert", "data", None)
    down_spec = P("expert", None, "data")
    wide_out = P(("rep", "expert"), "data", None)
    down_out = P(("rep", "expert"), None, "data")

    def y_perm(d):
        return [(z * 4 + y, z * 4 + (y + d) % 4) for z in range(4) for y in range(4)]

    def z_perm(d):
        return [(z * 4 + y, (z + d) % 4 * 4 + y) for z in range(4) for y in range(4)]

    perms = {"y": y_perm, "z": z_perm}
    partner = [(p, (p + n_pos // 2) % n_pos) for p in range(n_pos)]
    mate = [(p, p ^ 1) for p in range(n_pos)]
    to_neighbour = [(p, (p + (2 if p % 2 == 0 else -2)) % n_pos) for p in range(n_pos)]
    to_home = [(b, a) for a, b in to_neighbour]

    def step_along(v, axis, d):
        return lax.ppermute(v, "data", perms[axis](d))

    def gather_ring(v, axis, cut):
        one = step_along(v, axis, 1)
        three = step_along(v, axis, 3)
        two_a = step_along(one[:cut], axis, 1)
        two_b = step_along(three[cut:], axis, 3)
        return v, one, three, two_a, two_b

    def scatter_ring(parts, axis, cut):
        zero, one, three, two_a, two_b = parts
        in_a = step_along(two_a, axis, 1)
        in_b = step_along(two_b, axis, 3)
        one = one.at[:cut].add(in_a)
        three = three.at[cut:].add(in_b)
        return zero, step_along(one, axis, 1), step_along(three, axis, 3)

    def local_step(tok_in, expert_idx, gate_wt, w_gate, w_up, w_down, grad_out):
        tokens, top_k = expert_idx.shape
        width = tok_in.shape[1]
        n_loc, rows, f_dim = w_gate.shape
        n_exp = n_loc * n_pos
        cap = (5 * top_k * tokens + 4 * n_exp - 1) // (4 * n_exp)
        stride = ceil_to(cap, 16)
        half_n = n_loc // 2
        data_id = lax.axis_index("data")
        pos_id = lax.axis_index("expert")
        place = jnp.stack([data_id // 4, data_id % 4]).astype(jnp.int32)
        groups = jnp.stack([pos_id, (pos_id + n_pos // 2) % n_pos]).astype(jnp.int32)

        own = pack_weights(w_gate, w_up, jnp.swapaxes(w_down, 1, 2))
        other = lax.ppermute(own, "expert", partner)
        held = []
        for colour, (first, last) in enumerate((("y", "z"), ("z", "y"))):
            part = slice(colour * half_n, (colour + 1) * half_n)
            v = jnp.concatenate([own[part], other[part]], axis=0)
            v, one, three, two_a, two_b = gather_ring(v, first, half_n)
            four = jnp.stack([v, one, jnp.concatenate([two_a, two_b], axis=0), three])
            held.append(gather_ring(four, last, 2))

        gates = jnp.concatenate([gate_wt.reshape(-1), jnp.zeros((1024,), jnp.float32)])
        lists = make_list(expert_idx, cap, stride, n_loc)
        sets = [(tok_in, grad_out, gates, lists)]
        sets.append(tuple(lax.ppermute(a, "expert", mate) for a in sets[0]))
        sets.append(tuple(lax.ppermute(a, "expert", to_neighbour) for a in sets[0]))
        sets.append(tuple(lax.ppermute(a, "expert", mate) for a in sets[2]))
        sent = [dispatch(groups, li, g, x, d, stride, top_k, n_loc) for x, d, g, li in sets]
        r_sets, c_sets = [s[0] for s in sent], [s[1] for s in sent]

        prev = None
        grads = {}
        n_chunks = 2
        count = half_n // n_chunks
        for chunk in range(n_chunks):
            for colour in range(2):
                prev, parts = experts(place, r_sets, c_sets, held[colour], prev, colour, chunk * count, count, n_loc)
                first, last = ("y", "z") if colour == 0 else ("z", "y")
                zero, one, three = scatter_ring((parts[0], parts[1], parts[2], parts[3], parts[4]), first, 2)
                s = [zero[q] + one[q] + three[q] for q in range(4)]
                zero, one, three = scatter_ring((s[0], s[1], s[3], s[2][:count], s[2][count:]), last, count)
                mine = zero[:count] + one[:count] + three[:count]
                theirs = zero[count:] + one[count:] + three[count:]
                grads[colour, chunk] = (mine, lax.ppermute(theirs, "expert", partner))
        o_all, dr_all = prev

        sums = [combine(k, groups, sets[k][3], sets[k][2], o_all, dr_all, tokens, stride, top_k, n_loc) for k in (3, 2, 1, 0)][::-1]
        near = sums[2] + lax.ppermute(sums[3], "expert", mate)
        far = lax.ppermute(near, "expert", to_home)
        total = sums[0] + lax.ppermute(sums[1], "expert", mate) + far
        tok_out = (tok_in.astype(jnp.float32) + total[:, :width]).astype(jnp.bfloat16)
        grad_in = (grad_out.astype(jnp.float32) + total[:, width:]).astype(jnp.bfloat16)

        order = [grads[colour, chunk] for colour in range(2) for chunk in range(n_chunks)]
        gg, gu, gd = unpack_grads(order, n_loc, rows, f_dim)
        return tok_out, grad_in, gg, gu, jnp.swapaxes(gd, 1, 2)

    return jax.shard_map(local_step, mesh=mesh, in_specs=(row_spec, row_spec, row_spec, wide_spec, wide_spec, down_spec, row_spec), out_specs=(row_spec, row_spec, wide_out, wide_out, down_out), check_vma=False)
```

time: 1740 us -> 874 us (0.50)
  local copies, waits for them, and re-layouts: 967 us -> 20.1 us
  Pallas kernels: 0 us -> 488 us
  waiting for transfers between devices: 456 us -> 188 us
  matrix products: 174 us -> 0 us
  starting transfers between devices: 28.8 us -> 101 us
  other arithmetic: 96.2 us -> 61.4 us
    gather x41 -> x0, local copies, waits for them, and re-layouts: 867 us -> none  [the longest x5 432 us: gather_rows(): return jnp.take(table, index, axis=0, mode='fill', fill_value=0)]
    pallas_call x0 -> x16, Pallas kernels: none -> 488 us  [the longest x4 177 us: combine(): pl.pallas_call(functools.partial(combine_body, n_blk, stride, top_k, n_lo...]
    all_to_all x4 -> x0, waiting for transfers between devices: 362 us -> none  [the longest x1 131 us: local_step(): lax.all_to_all(exp_out, 'expert', 1, 1, tiled=True).reshape(-1, width)]
    ppermute x0 -> x68, waiting for transfers between devices: none -> 188 us  [the longest x48 145 us: step_along(): return lax.ppermute(v, 'data', perms[axis](d))]
    dot_general x9 -> x0, matrix products: 174 us -> none  [the longest x1 32.3 us: local_step(): jnp.einsum('lscd,ldf->lscf', recv_rows, wu_full, preferred_element_type=j...]
    ppermute x0 -> x68, starting transfers between devices: none -> 101 us  [the longest x48 54.9 us: step_along(): return lax.ppermute(v, 'data', perms[axis](d))]
    all_gather x3 -> x0, waiting for transfers between devices: 91.7 us -> none  [the longest x1 54.1 us: local_step(): wg_full = lax.all_gather(w_gate, 'data', axis=1, tiled=True)]
    reduce_sum x1 -> x0, other arithmetic: 46.2 us -> none  [local_step(): jnp.sum(pair_grad.astype(jnp.float32), axis=1)]
  transfers between devices with their start and end apart: 10 -> 68, of which waited for: 5 -> 21; matrix products, arithmetic and copies ran while one was open for 41% -> 7% of each run, Pallas kernels for 0% -> 42%
where the time goes in v1:
time: 874 us; the launch traced here: 860 us
  Pallas kernels  488 us (56%)
  waiting for transfers between devices  188 us (22%)
  starting transfers between devices  101 us (12%)
  other arithmetic  61.4 us (7%)
  local copies, waits for them, and re-layouts  20.1 us (2%)
    pallas_call x4, Pallas kernels, combine(): pl.pallas_call(functools.partial(combine_body, n_blk, stride, top_k, n_lo...  177 us
    pallas_call x4, Pallas kernels, dispatch(): pl.pallas_call(functools.partial(dispatch_body, n_blk, stride, top_k, n_l...  165 us
    ppermute x48, waiting for transfers between devices, step_along(): return lax.ppermute(v, 'data', perms[axis](d))  145 us
    pallas_call x4, Pallas kernels, experts(): pl.pallas_call(functools.partial(experts_body, n_sets, last, first, prev...  107 us
    ppermute x48, starting transfers between devices, step_along(): return lax.ppermute(v, 'data', perms[axis](d))  54.9 us
    ppermute x4, waiting for transfers between devices, local_step(): lax.ppermute(a, 'expert', to_neighbour)  30.9 us
    pallas_call x1, Pallas kernels, make_list(): pl.pallas_call(functools.partial(list_body, top_k, tokens), out_shape=jax...  30 us
    ppermute x4, starting transfers between devices, local_step(): grads[colour, chunk] = (mine, lax.ppermute(theirs, 'expert', partner))  23.3 us
  transfers between devices with their start and end apart: 68, of which 21 were waited for; matrix products, arithmetic and copies ran while one was open for 7% of the time, Pallas kernels for 42%

profile of v1, /device:TPU:1, one launch (start us, length us, event | category | flops | bytes accessed | tf_op | source)
XLA Modules:
  0.0 860.0 jit_solution(7422728405755094568)
XLA Ops:
  2.7 3.6 collective-permute-start.12
  7.4 11.6 %collective-permute-done.12 = bf16[16,144,128]{2,1,0:T(8,128)(2,1)S(1)} collective-permute-done((bf16[16,144,128]{2,1,0:T(8,128)(2,1)}, bf16[16,144,128]{2,1,0:T(8,128)(2,1)S(1)}, u32[]{:S(2)}, u32[]{:S(2)}) %collective-permute-start.12) | collective-permute-done | bytes 589856 | tf_op jit(solution)/shard_map/ppermute | solution.py:499
  22.9 3.7 route.1
  39.7 30.0 %lists.1.list_ref = s32[25600]{0:T(1024)} custom-call(s32[25600]{0:T(1024)} %broadcast_in_dim.4.fill_ref, s32[16384]{0:T(1024)} %bitcast.137), custom_call_target="tpu_custom_call" | custom-call | flops 10000000000 | bytes 131072 | tf_op jit(solution)/shard_map/lists/pallas_call | solution.py:76
  82.7 3.7 collective-permute-start.16
  94.8 11.1 %collective-permute-done.6.x_ref = bf16[2048,512]{1,0:T(8,128)(2,1)S(1)} collective-permute-done((bf16[2048,512]{1,0:T(8,128)(2,1)S(1)}, bf16[2048,512]{1,0:T(8,128)(2,1)S(1)}, u32[]{:S(2)}, u32[]{:S(2)}) %collective-permute-start.6) | collective-permute-done | bytes 2097184 | tf_op jit(solution)/shard_map/ppermute | solution.py:512
  108.6 19.8 %collective-permute-done.7.dy_ref = bf16[2048,512]{1,0:T(8,128)(2,1)} collective-permute-done((bf16[2048,512]{1,0:T(8,128)(2,1)}, bf16[2048,512]{1,0:T(8,128)(2,1)}, u32[]{:S(2)}, u32[]{:S(2)}) %collective-permute-start.7) | collective-permute-done | bytes 2097184 | tf_op jit(solution)/shard_map/ppermute | solution.py:512
  132.0 11.2 %collective-permute-done.26.refs_11_ = bf16[4,16,144,128]{3,2,1,0:T(8,128)(2,1)} collective-permute-done((bf16[4,16,144,128]{3,2,1,0:T(8,128)(2,1)}, bf16[4,16,144,128]{3,2,1,0:T(8,128)(2,1)}, u32[]{:S(2)}, u32[]{:S(2)}) %collective-permute-start.26) | collective-permute-done | bytes 2359328 | tf_op jit(solution)/shard_map/ppermute | solution.py:468
  144.9 41.2 %dispatch.4 = (bf16[32,160,512]{2,1,0:T(8,128)(2,1)}, bf16[32,160,512]{2,1,0:T(8,128)(2,1)}) custom-call(s32[2]{0:T(128)} %pad_add_fusion.groups_ref, s32[25600]{0:T(1024)} %lists.1.list_ref, f32[17408]{0:T(1024)} %copy-done.16, bf16[2048,512]{1,0:T(8,128)(2,1)} %x_ref.1, bf16[2048,512]{1,0:T(8,128)(2,1)} %dy_ref.1), custom_call_target="tpu_custom_call" | custom-call | flops 10000000000 | bytes 16777216 | tf_op jit(solution)/shard_map/dispatch/pallas_call | solution.py:144
  186.7 41.2 %dispatch.6 = (bf16[32,160,512]{2,1,0:T(8,128)(2,1)}, bf16[32,160,512]{2,1,0:T(8,128)(2,1)}) custom-call(s32[2]{0:T(128)} %pad_add_fusion.groups_ref, s32[25600]{0:T(1024)} %collective-permute-done.4.list_ref, f32[17408]{0:T(1024)} %copy-done.29, bf16[2048,512]{1,0:T(8,128)(2,1)} %copy-done.17, bf16[2048,512]{1,0:T(8,128)(2,1)} %collective-permute-done.7.dy_ref), custom_call_target="tpu_custom_call" | custom-call | flops 10000000000 | bytes 16777216 | tf_op jit(solution)/shard_map/dispatch/pallas_call | solution.py:144
  234.9 41.3 %dispatch.5 = (bf16[32,160,512]{2,1,0:T(8,128)(2,1)}, bf16[32,160,512]{2,1,0:T(8,128)(2,1)}) custom-call(s32[2]{0:T(128)} %pad_add_fusion.groups_ref, s32[25600]{0:T(1024)} %collective-permute-done.list_ref, f32[17408]{0:T(1024)} %copy-done.30, bf16[2048,512]{1,0:T(8,128)(2,1)} %copy-done.18, bf16[2048,512]{1,0:T(8,128)(2,1)} %collective-permute-done.3.dy_ref), custom_call_target="tpu_custom_call" | custom-call | flops 10000000000 | bytes 16777216 | tf_op jit(solution)/shard_map/dispatch/pallas_call | solution.py:144
  282.8 41.2 %dispatch.7 = (bf16[32,160,512]{2,1,0:T(8,128)(2,1)}, bf16[32,160,512]{2,1,0:T(8,128)(2,1)}) custom-call(s32[2]{0:T(128)} %pad_add_fusion.groups_ref, s32[25600]{0:T(1024)} %collective-permute-done.8.list_ref, f32[17408]{0:T(1024)} %copy-done.31, bf16[2048,512]{1,0:T(8,128)(2,1)} %collective-permute-done.10.x_ref, ...), custom_call_target="tpu_custom_call" | custom-call | flops 10000000000 | bytes 16777216 | tf_op jit(solution)/shard_map/dispatch/pallas_call | solution.py:144
  324.1 26.8 %experts.4 = (bf16[4,32,160,512]{3,2,1,0:T(8,128)(2,1)}, bf16[4,32,160,512]{3,2,1,0:T(8,128)(2,1)}, f32[4,8,144,128]{3,2,1,0:T(8,128)}, f32[4,8,144,128]{3,2,1,0...) custom-call(s32[2]{0:T(128)} %pad_add_fusion.1.refs_0_, ...), custom_call_target="tpu_custom_call" | custom-call | flops 24000000000 | bytes 48000000 | tf_op jit(solution)/shard_map/experts/pallas_call | solution.py:422
  352.3 26.8 %experts.5 = (bf16[4,32,160,512]{3,2,1,0:T(8,128)(2,1)}, bf16[4,32,160,512]{3,2,1,0:T(8,128)(2,1)}, f32[4,8,144,128]{3,2,1,0:T(8,128)}, f32[4,8,144,128]{3,2,1,0...) custom-call(s32[2]{0:T(128)} %pad_add_fusion.1.refs_0_, ...), custom_call_target="tpu_custom_call", output_to_operand_aliasing={{0}: (14, {}), {1}: (15, {})} | custom-call | flops 24000000000 | bytes 48000000 | tf_op jit(solution)/shard_map/experts/pallas_call | solution.py:422
  379.2 26.8 %experts.6 = (bf16[4,32,160,512]{3,2,1,0:T(8,128)(2,1)}, bf16[4,32,160,512]{3,2,1,0:T(8,128)(2,1)}, f32[4,8,144,128]{3,2,1,0:T(8,128)}, f32[4,8,144,128]{3,2,1,0...) custom-call(s32[2]{0:T(128)} %pad_add_fusion.1.refs_0_, ...), custom_call_target="tpu_custom_call", output_to_operand_aliasing={{0}: (14, {}), {1}: (15, {})} | custom-call | flops 24000000000 | bytes 48000000 | tf_op jit(solution)/shard_map/experts/pallas_call | solution.py:422
  406.0 26.8 %experts.7 = (bf16[4,32,160,512]{3,2,1,0:T(8,128)(2,1)}, bf16[4,32,160,512]{3,2,1,0:T(8,128)(2,1)}, f32[4,8,144,128]{3,2,1,0:T(8,128)}, f32[4,8,144,128]{3,2,1,0...) custom-call(s32[2]{0:T(128)} %pad_add_fusion.1.refs_0_, ...), custom_call_target="tpu_custom_call", output_to_operand_aliasing={{0}: (14, {}), {1}: (15, {})} | custom-call | flops 24000000000 | bytes 48000000 | tf_op jit(solution)/shard_map/experts/pallas_call | solution.py:422
  432.9 44.4 %combine.7 = f32[2048,1024]{1,0:T(8,128)} custom-call(s32[2]{0:T(128)} %pad_add_fusion.groups_ref, s32[25600]{0:T(1024)} %collective-permute-done.8.list_ref, f32[17408]{0:T(1024)} %copy-done.31, bf16[4,32,160,512]{3,2,1,0:T(8,128)(2,1)} %get-tuple-element.250.o_ref, bf16[4,32,160,512]{3,2,1,0:T(8,128)(2,1)} %get-tuple-element.251.dr_ref), custom_call_target="tpu_custom_call" | custom-call | flops 14000000000 | bytes 16777216 | tf_op jit(solution)/shard_map/combine/pallas_call | solution.py:227
  481.4 25.5 %collective-permute-done.32 = f32[2,8,144,128]{3,2,1,0:T(8,128)S(1)} collective-permute-done((f32[2,8,144,128]{3,2,1,0:T(8,128)}, f32[2,8,144,128]{3,2,1,0:T(8,128)S(1)}, u32[]{:S(2)}, u32[]{:S(2)}) %collective-permute-start.32) | collective-permute-done | bytes 1179680 | tf_op jit(solution)/shard_map/ppermute | solution.py:468
  512.3 18.9 %collective-permute-done.43 = f32[2,8,144,128]{3,2,1,0:T(8,128)S(1)} collective-permute-done((f32[2,8,144,128]{3,2,1,0:T(8,128)}, f32[2,8,144,128]{3,2,1,0:T(8,128)S(1)}, u32[]{:S(2)}, u32[]{:S(2)}) %collective-permute-start.43) | collective-permute-done | bytes 1179680 | tf_op jit(solution)/shard_map/ppermute | solution.py:468
  547.4 12.4 %collective-permute-done.61 = f32[2,8,144,128]{3,2,1,0:T(8,128)} collective-permute-done((f32[2,8,144,128]{3,2,1,0:T(8,128)S(1)}, f32[2,8,144,128]{3,2,1,0:T(8,128)}, u32[]{:S(2)}, u32[]{:S(2)}) %collective-permute-start.61) | collective-permute-done | bytes 1179680 | tf_op jit(solution)/shard_map/ppermute | solution.py:468
  565.2 44.2 %combine.6 = f32[2048,1024]{1,0:T(8,128)} custom-call(s32[2]{0:T(128)} %pad_add_fusion.groups_ref, s32[25600]{0:T(1024)} %collective-permute-done.4.list_ref, f32[17408]{0:T(1024)} %copy-done.29, bf16[4,32,160,512]{3,2,1,0:T(8,128)(2,1)} %get-tuple-element.250.o_ref, bf16[4,32,160,512]{3,2,1,0:T(8,128)(2,1)} %get-tuple-element.251.dr_ref), custom_call_target="tpu_custom_call" | custom-call | flops 14000000000 | bytes 16777216 | tf_op jit(solution)/shard_map/combine/pallas_call | solution.py:227
  609.5 44.1 %combine.5 = f32[2048,1024]{1,0:T(8,128)} custom-call(s32[2]{0:T(128)} %pad_add_fusion.groups_ref, s32[25600]{0:T(1024)} %collective-permute-done.list_ref, f32[17408]{0:T(1024)} %copy-done.30, bf16[4,32,160,512]{3,2,1,0:T(8,128)(2,1)} %get-tuple-element.250.o_ref, bf16[4,32,160,512]{3,2,1,0:T(8,128)(2,1)} %get-tuple-element.251.dr_ref), custom_call_target="tpu_custom_call" | custom-call | flops 14000000000 | bytes 16777216 | tf_op jit(solution)/shard_map/combine/pallas_call | solution.py:227
  653.6 12.3 %add.336 = f32[2048,1024]{1,0:T(8,128)} add(f32[2048,1024]{1,0:T(8,128)} %combine.6, f32[2048,1024]{1,0:T(8,128)} %collective-permute-done.30) | non-fusion elementwise | flops 2097152 | bytes 25165824 | tf_op jit(solution)/shard_map/add | solution.py:534
  681.3 41.5 %collective-permute-done.42 = f32[4,8,144,128]{3,2,1,0:T(8,128)S(1)} collective-permute-done((f32[4,8,144,128]{3,2,1,0:T(8,128)S(1)}, f32[4,8,144,128]{3,2,1,0:T(8,128)S(1)}, u32[]{:S(2)}, u32[]{:S(2)}) %collective-permute-start.42) | collective-permute-done | bytes 2359328 | tf_op jit(solution)/shard_map/ppermute | solution.py:468
  728.6 5.4 collective-permute-done.36
  750.4 5.1 collective-permute-done.39
  761.4 3.9 collective-permute-done.55
  771.6 13.1 %collective-permute-start.40 = (f32[4,144,128]{2,1,0:T(8,128)S(1)}, f32[4,144,128]{2,1,0:T(8,128)S(1)}, u32[]{:S(2)}, u32[]{:S(2)}) collective-permute-start(f32[4,144,128]{2,1,0:T(8,128)S(1)} %get-tuple-element.299), channel_id=1, source_target_pairs={{0,4},{1,5},{2,6},{3,7},{4,0},{5,1},{6,2},{7,3},{8,12},{9,13},{10,... | collective-permute-start | bytes 884744 | tf_op jit(solution)/shard_map/ppermute | solution.py:530
  788.9 6.6 collective-permute-start.49
  796.5 44.2 %combine.4 = f32[2048,1024]{1,0:T(8,128)} custom-call(s32[2]{0:T(128)} %pad_add_fusion.groups_ref, s32[25600]{0:T(1024)} %lists.1.list_ref, f32[17408]{0:T(1024)} %copy-done.16, bf16[4,32,160,512]{3,2,1,0:T(8,128)(2,1)} %get-tuple-element.250.o_ref, bf16[4,32,160,512]{3,2,1,0:T(8,128)(2,1)} %get-tuple-element.251.dr_ref), custom_call_target="tpu_custom_call" | custom-call | flops 14000000000 | bytes 16777216 | tf_op jit(solution)/shard_map/combine/pallas_call | solution.py:227
  844.5 9.9 %add_add_fusion = f32[2048,1024]{1,0:T(8,128)S(1)} fusion(f32[2048,1024]{1,0:T(8,128)} %collective-permute-done.31, f32[2048,1024]{1,0:T(8,128)} %combine.4, f32[2048,1024]{1,0:T(8,128)} %collective-permute-done.29), kind=kLoop, calls=%fused_computation | loop fusion | flops 4194304 | bytes 33554432 | tf_op jit(solution)/shard_map/add | solution.py:536
  854.4 5.1 fusion
  (246 shorter events, 154.4 us)
Async XLA Ops:
  29.0 44.7 %collective-permute-start.13 = (bf16[16,144,128]{2,1,0:T(8,128)(2,1)}, bf16[16,144,128]{2,1,0:T(8,128)(2,1)S(1)}, u32[]{:S(2)}, u32[]{:S(2)}) collective-permute-start(bf16[16,144,128]{2,1,0:T(8,128)(2,1)} %get-tuple-element.316), channel_id=1, source_target_pairs={{0,32},{8,40},{16,48},{24,56},{32,64},{40,72},{48,80},{56,88},{64,... | collective-permute-start | bytes 1769480 | tf_op jit(solution)/shard_map/ppermute | solution.py:468
  30.7 45.4 %collective-permute-start.15 = (bf16[16,144,128]{2,1,0:T(8,128)(2,1)}, bf16[16,144,128]{2,1,0:T(8,128)(2,1)S(1)}, u32[]{:S(2)}, u32[]{:S(2)}) collective-permute-start(bf16[16,144,128]{2,1,0:T(8,128)(2,1)} %get-tuple-element.316), channel_id=1, source_target_pairs={{0,96},{8,104},{16,112},{24,120},{32,0},{40,8},{48,16},{56,24},{64... | collective-permute-start | bytes 1769480 | tf_op jit(solution)/shard_map/ppermute | solution.py:468
  35.6 42.0 %collective-permute-start.22 = (bf16[8,144,128]{2,1,0:T(8,128)(2,1)}, bf16[8,144,128]{2,1,0:T(8,128)(2,1)}, u32[]{:S(2)}, u32[]{:S(2)}) collective-permute-start(bf16[8,144,128]{2,1,0:T(8,128)(2,1)} %slice.896), channel_id=1, source_target_pairs={{0,8},{8,16},{16,24},{24,0},{32,40},{40,48},{48,56},{56,32},{64,72... | collective-permute-start | bytes 884744 | tf_op jit(solution)/shard_map/ppermute | solution.py:468
  36.4 41.3 %collective-permute-start.24 = (bf16[8,144,128]{2,1,0:T(8,128)(2,1)}, bf16[8,144,128]{2,1,0:T(8,128)(2,1)}, u32[]{:S(2)}, u32[]{:S(2)}) collective-permute-start(bf16[8,144,128]{2,1,0:T(8,128)(2,1)} %slice.897), channel_id=1, source_target_pairs={{0,24},{8,0},{16,8},{24,16},{32,56},{40,32},{48,40},{56,48},{64,88... | collective-permute-start | bytes 884744 | tf_op jit(solution)/shard_map/ppermute | solution.py:468
  89.3 53.9 %collective-permute-start.26 = (bf16[4,16,144,128]{3,2,1,0:T(8,128)(2,1)}, bf16[4,16,144,128]{3,2,1,0:T(8,128)(2,1)}, u32[]{:S(2)}, u32[]{:S(2)}) collective-permute-start(bf16[4,16,144,128]{3,2,1,0:T(8,128)(2,1)} %pad_maximum_fusion.1.refs_9_), channel_id=1, source_target_pairs={{0,96},{8,104},{16,112},{24,120},{32,0},{40,8},{48,16},{56,24},{64... | collective-permute-start | bytes 7077896 | tf_op jit(solution)/shard_map/ppermute | solution.py:468
  90.0 54.1 %collective-permute-start.25 = (bf16[4,16,144,128]{3,2,1,0:T(8,128)(2,1)}, bf16[4,16,144,128]{3,2,1,0:T(8,128)(2,1)}, u32[]{:S(2)}, u32[]{:S(2)}) collective-permute-start(bf16[4,16,144,128]{3,2,1,0:T(8,128)(2,1)} %pad_maximum_fusion.1.refs_9_), channel_id=1, source_target_pairs={{0,32},{8,40},{16,48},{24,56},{32,64},{40,72},{48,80},{56,88},{64,... | collective-permute-start | bytes 7077896 | tf_op jit(solution)/shard_map/ppermute | solution.py:468
  105.9 125.8 %collective-permute-start.18 = (bf16[4,16,144,128]{3,2,1,0:T(8,128)(2,1)S(1)}, bf16[4,16,144,128]{3,2,1,0:T(8,128)(2,1)}, u32[]{:S(2)}, u32[]{:S(2)}) collective-permute-start(bf16[4,16,144,128]{3,2,1,0:T(8,128)(2,1)S(1)} %pad_maximum_fusion.refs_9_), channel_id=1, source_target_pairs={{0,24},{8,0},{16,8},{24,16},{32,56},{40,32},{48,40},{56,48},{64,88... | collective-permute-start | bytes 7077896 | tf_op jit(solution)/shard_map/ppermute | solution.py:468
  107.2 127.7 %collective-permute-start.17 = (bf16[4,16,144,128]{3,2,1,0:T(8,128)(2,1)S(1)}, bf16[4,16,144,128]{3,2,1,0:T(8,128)(2,1)}, u32[]{:S(2)}, u32[]{:S(2)}) collective-permute-start(bf16[4,16,144,128]{3,2,1,0:T(8,128)(2,1)S(1)} %pad_maximum_fusion.refs_9_), channel_id=1, source_target_pairs={{0,8},{8,16},{16,24},{24,0},{32,40},{40,48},{48,56},{56,32},{64,72... | collective-permute-start | bytes 7077896 | tf_op jit(solution)/shard_map/ppermute | solution.py:468
  128.4 103.3 %collective-permute-start.3 = (bf16[2048,512]{1,0:T(8,128)(2,1)}, bf16[2048,512]{1,0:T(8,128)(2,1)}, u32[]{:S(2)}, u32[]{:S(2)}) collective-permute-start(bf16[2048,512]{1,0:T(8,128)(2,1)} %dy_ref.1), channel_id=1, source_target_pairs={{0,1},{1,0},{2,3},{3,2},{4,5},{5,4},{6,7},{7,6},{8,9},{9,8},{10,11... | collective-permute-start | bytes 6291464 | tf_op jit(solution)/shard_map/ppermute | solution.py:511
  143.2 138.0 %collective-permute-start.10 = (bf16[2048,512]{1,0:T(8,128)(2,1)}, bf16[2048,512]{1,0:T(8,128)(2,1)}, u32[]{:S(2)}, u32[]{:S(2)}) collective-permute-start(bf16[2048,512]{1,0:T(8,128)(2,1)} %copy-done.17), channel_id=1, source_target_pairs={{0,1},{1,0},{2,3},{3,2},{4,5},{5,4},{6,7},{7,6},{8,9},{9,8},{10,11... | collective-permute-start | bytes 6291464 | tf_op jit(solution)/shard_map/ppermute | solution.py:513
  144.1 138.7 %collective-permute-start.11 = (bf16[2048,512]{1,0:T(8,128)(2,1)}, bf16[2048,512]{1,0:T(8,128)(2,1)}, u32[]{:S(2)}, u32[]{:S(2)}) collective-permute-start(bf16[2048,512]{1,0:T(8,128)(2,1)} %collective-permute-done.7.dy_ref), channel_id=1, source_target_pairs={{0,1},{1,0},{2,3},{3,2},{4,5},{5,4},{6,7},{7,6},{8,9},{9,8},{10,11... | collective-permute-start | bytes 6291464 | tf_op jit(solution)/shard_map/ppermute | solution.py:513
  231.7 49.3 %collective-permute-start.8 = (s32[25600]{0:T(1024)}, s32[25600]{0:T(1024)}, u32[]{:S(2)}, u32[]{:S(2)}) collective-permute-start(s32[25600]{0:T(1024)} %collective-permute-done.4.list_ref), channel_id=1, source_target_pairs={{0,1},{1,0},{2,3},{3,2},{4,5},{5,4},{6,7},{7,6},{8,9},{9,8},{10,11... | collective-permute-start | bytes 307208 | tf_op jit(solution)/shard_map/ppermute | solution.py:513
  231.8 92.3 %collective-permute-start.28 = (bf16[2,16,144,128]{3,2,1,0:T(8,128)(2,1)}, bf16[2,16,144,128]{3,2,1,0:T(8,128)(2,1)}, u32[]{:S(2)}, u32[]{:S(2)}) collective-permute-start(bf16[2,16,144,128]{3,2,1,0:T(8,128)(2,1)} %slice.899), channel_id=1, source_target_pairs={{0,96},{8,104},{16,112},{24,120},{32,0},{40,8},{48,16},{56,24},{64... | collective-permute-start | bytes 3538952 | tf_op jit(solution)/shard_map/ppermute | solution.py:468
  234.9 89.1 %collective-permute-start.27 = (bf16[2,16,144,128]{3,2,1,0:T(8,128)(2,1)S(1)}, bf16[2,16,144,128]{3,2,1,0:T(8,128)(2,1)}, u32[]{:S(2)}, u32[]{:S(2)}) collective-permute-start(bf16[2,16,144,128]{3,2,1,0:T(8,128)(2,1)S(1)} %slice.898), channel_id=1, source_target_pairs={{0,32},{8,40},{16,48},{24,56},{32,64},{40,72},{48,80},{56,88},{64,... | collective-permute-start | bytes 3538952 | tf_op jit(solution)/shard_map/ppermute | solution.py:468
  281.0 70.0 %collective-permute-start.20 = (bf16[2,16,144,128]{3,2,1,0:T(8,128)(2,1)}, bf16[2,16,144,128]{3,2,1,0:T(8,128)(2,1)S(1)}, u32[]{:S(2)}, u32[]{:S(2)}) collective-permute-start(bf16[2,16,144,128]{3,2,1,0:T(8,128)(2,1)} %slice.893), channel_id=1, source_target_pairs={{0,24},{8,0},{16,8},{24,16},{32,56},{40,32},{48,40},{56,48},{64,88... | collective-permute-start | bytes 3538952 | tf_op jit(solution)/shard_map/ppermute | solution.py:468
  281.2 69.7 %collective-permute-start.19 = (bf16[2,16,144,128]{3,2,1,0:T(8,128)(2,1)}, bf16[2,16,144,128]{3,2,1,0:T(8,128)(2,1)S(1)}, u32[]{:S(2)}, u32[]{:S(2)}) collective-permute-start(bf16[2,16,144,128]{3,2,1,0:T(8,128)(2,1)} %slice.892), channel_id=1, source_target_pairs={{0,8},{8,16},{16,24},{24,0},{32,40},{40,48},{48,56},{56,32},{64,72... | collective-permute-start | bytes 3538952 | tf_op jit(solution)/shard_map/ppermute | solution.py:468
  477.3 86.1 %collective-permute-start.30 = (f32[2048,1024]{1,0:T(8,128)}, f32[2048,1024]{1,0:T(8,128)}, u32[]{:S(2)}, u32[]{:S(2)}) collective-permute-start(f32[2048,1024]{1,0:T(8,128)} %combine.7), channel_id=1, source_target_pairs={{0,1},{1,0},{2,3},{3,2},{4,5},{5,4},{6,7},{7,6},{8,9},{9,8},{10,11... | collective-permute-start | bytes 25165832 | tf_op jit(solution)/shard_map/ppermute | solution.py:534
  481.0 50.2 %collective-permute-start.43 = (f32[2,8,144,128]{3,2,1,0:T(8,128)}, f32[2,8,144,128]{3,2,1,0:T(8,128)S(1)}, u32[]{:S(2)}, u32[]{:S(2)}) collective-permute-start(f32[2,8,144,128]{3,2,1,0:T(8,128)} %get-tuple-element.261), channel_id=1, source_target_pairs={{0,24},{8,0},{16,8},{24,16},{32,56},{40,32},{48,40},{56,48},{64,88... | collective-permute-start | bytes 3538952 | tf_op jit(solution)/shard_map/ppermute | solution.py:468
  481.2 52.9 %collective-permute-start.50 = (f32[2,8,144,128]{3,2,1,0:T(8,128)S(1)}, f32[2,8,144,128]{3,2,1,0:T(8,128)S(1)}, u32[]{:S(2)}, u32[]{:S(2)}) collective-permute-start(f32[2,8,144,128]{3,2,1,0:T(8,128)S(1)} %copy-done.23), channel_id=1, source_target_pairs={{0,32},{8,40},{16,48},{24,56},{32,64},{40,72},{48,80},{56,88},{64,... | collective-permute-start | bytes 3538952 | tf_op jit(solution)/shard_map/ppermute | solution.py:468
  542.3 123.6 %collective-permute-start.35 = (f32[4,8,144,128]{3,2,1,0:T(8,128)}, f32[4,8,144,128]{3,2,1,0:T(8,128)S(1)}, u32[]{:S(2)}, u32[]{:S(2)}) collective-permute-start(f32[4,8,144,128]{3,2,1,0:T(8,128)} %add_dynamic-update-slice_fusion.6), channel_id=1, source_target_pairs={{0,24},{8,0},{16,8},{24,16},{32,56},{40,32},{48,40},{56,48},{64,88... | collective-permute-start | bytes 7077896 | tf_op jit(solution)/shard_map/ppermute | solution.py:468
  547.4 121.4 %collective-permute-start.33 = (f32[4,8,144,128]{3,2,1,0:T(8,128)}, f32[4,8,144,128]{3,2,1,0:T(8,128)}, u32[]{:S(2)}, u32[]{:S(2)}) collective-permute-start(f32[4,8,144,128]{3,2,1,0:T(8,128)} %add_dynamic-update-slice_fusion.7), channel_id=1, source_target_pairs={{0,8},{8,16},{16,24},{24,0},{32,40},{40,48},{48,56},{56,32},{64,72... | collective-permute-start | bytes 7077896 | tf_op jit(solution)/shard_map/ppermute | solution.py:468
  559.9 111.0 %collective-permute-start.53 = (f32[4,8,144,128]{3,2,1,0:T(8,128)}, f32[4,8,144,128]{3,2,1,0:T(8,128)}, u32[]{:S(2)}, u32[]{:S(2)}) collective-permute-start(f32[4,8,144,128]{3,2,1,0:T(8,128)} %add_dynamic-update-slice_fusion.2), channel_id=1, source_target_pairs={{0,96},{8,104},{16,112},{24,120},{32,0},{40,8},{48,16},{56,24},{64... | collective-permute-start | bytes 7077896 | tf_op jit(solution)/shard_map/ppermute | solution.py:468
  563.4 109.2 %collective-permute-start.51 = (f32[4,8,144,128]{3,2,1,0:T(8,128)}, f32[4,8,144,128]{3,2,1,0:T(8,128)}, u32[]{:S(2)}, u32[]{:S(2)}) collective-permute-start(f32[4,8,144,128]{3,2,1,0:T(8,128)} %add_dynamic-update-slice_fusion.3), channel_id=1, source_target_pairs={{0,32},{8,40},{16,48},{24,56},{32,64},{40,72},{48,80},{56,88},{64,... | collective-permute-start | bytes 7077896 | tf_op jit(solution)/shard_map/ppermute | solution.py:468
  563.4 112.5 %collective-permute-start.44 = (f32[4,8,144,128]{3,2,1,0:T(8,128)}, f32[4,8,144,128]{3,2,1,0:T(8,128)}, u32[]{:S(2)}, u32[]{:S(2)}) collective-permute-start(f32[4,8,144,128]{3,2,1,0:T(8,128)} %add_dynamic-update-slice_fusion.4), channel_id=1, source_target_pairs={{0,24},{8,0},{16,8},{24,16},{32,56},{40,32},{48,40},{56,48},{64,88... | collective-permute-start | bytes 7077896 | tf_op jit(solution)/shard_map/ppermute | solution.py:468
  665.9 178.6 %collective-permute-start.29 = (f32[2048,1024]{1,0:T(8,128)}, f32[2048,1024]{1,0:T(8,128)}, u32[]{:S(2)}, u32[]{:S(2)}) collective-permute-start(f32[2048,1024]{1,0:T(8,128)} %combine.5), channel_id=1, source_target_pairs={{0,1},{1,0},{2,3},{3,2},{4,5},{5,4},{6,7},{7,6},{8,9},{9,8},{10,11... | collective-permute-start | bytes 25165832 | tf_op jit(solution)/shard_map/ppermute | solution.py:536
  668.9 175.7 %collective-permute-start.31 = (f32[2048,1024]{1,0:T(8,128)}, f32[2048,1024]{1,0:T(8,128)}, u32[]{:S(2)}, u32[]{:S(2)}) collective-permute-start(f32[2048,1024]{1,0:T(8,128)} %add.336), channel_id=1, source_target_pairs={{2,0},{7,1},{4,2},{1,3},{6,4},{3,5},{0,6},{5,7},{10,8},{15,9},{12,... | collective-permute-start | bytes 25165832 | tf_op jit(solution)/shard_map/ppermute | solution.py:535
  670.9 52.0 %collective-permute-start.42 = (f32[4,8,144,128]{3,2,1,0:T(8,128)S(1)}, f32[4,8,144,128]{3,2,1,0:T(8,128)S(1)}, u32[]{:S(2)}, u32[]{:S(2)}) collective-permute-start(f32[4,8,144,128]{3,2,1,0:T(8,128)S(1)} %add_dynamic-update-slice_fusion.5), channel_id=1, source_target_pairs={{0,8},{8,16},{16,24},{24,0},{32,40},{40,48},{48,56},{56,32},{64,72... | collective-permute-start | bytes 7077896 | tf_op jit(solution)/shard_map/ppermute | solution.py:468
  672.7 52.3 %collective-permute-start.62 = (f32[4,8,144,128]{3,2,1,0:T(8,128)S(1)}, f32[4,8,144,128]{3,2,1,0:T(8,128)S(1)}, u32[]{:S(2)}, u32[]{:S(2)}) collective-permute-start(f32[4,8,144,128]{3,2,1,0:T(8,128)S(1)} %add_dynamic-update-slice_fusion), channel_id=1, source_target_pairs={{0,96},{8,104},{16,112},{24,120},{32,0},{40,8},{48,16},{56,24},{64... | collective-permute-start | bytes 7077896 | tf_op jit(solution)/shard_map/ppermute | solution.py:468
  676.0 52.2 %collective-permute-start.60 = (f32[4,8,144,128]{3,2,1,0:T(8,128)S(1)}, f32[4,8,144,128]{3,2,1,0:T(8,128)S(1)}, u32[]{:S(2)}, u32[]{:S(2)}) collective-permute-start(f32[4,8,144,128]{3,2,1,0:T(8,128)S(1)} %add_dynamic-update-slice_fusion.1), channel_id=1, source_target_pairs={{0,32},{8,40},{16,48},{24,56},{32,64},{40,72},{48,80},{56,88},{64,... | collective-permute-start | bytes 7077896 | tf_op jit(solution)/shard_map/ppermute | solution.py:468
  785.6 55.1 %collective-permute-start.58 = (f32[4,144,128]{2,1,0:T(8,128)S(1)}, f32[4,144,128]{2,1,0:T(8,128)S(1)}, u32[]{:S(2)}, u32[]{:S(2)}) collective-permute-start(f32[4,144,128]{2,1,0:T(8,128)S(1)} %get-tuple-element.295), channel_id=1, source_target_pairs={{0,4},{1,5},{2,6},{3,7},{4,0},{5,1},{6,2},{7,3},{8,12},{9,13},{10,... | collective-permute-start | bytes 884744 | tf_op jit(solution)/shard_map/ppermute | solution.py:530
  788.9 51.9 %collective-permute-start.49 = (f32[4,144,128]{2,1,0:T(8,128)S(1)}, f32[4,144,128]{2,1,0:T(8,128)S(1)}, u32[]{:S(2)}, u32[]{:S(2)}) collective-permute-start(f32[4,144,128]{2,1,0:T(8,128)S(1)} %get-tuple-element.297), channel_id=1, source_target_pairs={{0,4},{1,5},{2,6},{3,7},{4,0},{5,1},{6,2},{7,3},{8,12},{9,13},{10,... | collective-permute-start | bytes 884744 | tf_op jit(solution)/shard_map/ppermute | solution.py:530
  796.3 44.5 %collective-permute-start.67 = (f32[4,144,128]{2,1,0:T(8,128)S(1)}, f32[4,144,128]{2,1,0:T(8,128)S(1)}, u32[]{:S(2)}, u32[]{:S(2)}) collective-permute-start(f32[4,144,128]{2,1,0:T(8,128)S(1)} %get-tuple-element.293), channel_id=1, source_target_pairs={{0,4},{1,5},{2,6},{3,7},{4,0},{5,1},{6,2},{7,3},{8,12},{9,13},{10,... | collective-permute-start | bytes 884744 | tf_op jit(solution)/shard_map/ppermute | solution.py:530
  (68 other events, 1231.1 us)

commit v2 on v1

--- a/solution.py
+++ b/solution.py
@@ -9,7 +9,7 @@
 
 
 LANES = 128
-GROUP = 3072
+TAIL = 1024
 VMEM_BIG = 60 * 1024 * 1024
 
 
@@ -17,83 +17,52 @@
     return (n + m - 1) // m * m
 
 
-def call(body, interpret=False, **kw):
-    return pl.pallas_call(body, **kw)
-
-
-def route_body(cap, stride, n_loc, ids_ref, dest_ref):
+def starts_body(ids_ref, out_ref):
     top_k, tokens = ids_ref.shape
-    n_exp = 128
     blk = min(256, tokens)
-    before = (lax.broadcasted_iota(jnp.int32, (blk, blk), 0) < lax.broadcasted_iota(jnp.int32, (blk, blk), 1)).astype(jnp.bfloat16)
-    exp_iota = lax.broadcasted_iota(jnp.int32, (n_exp, blk), 0)
-    n_pos = n_exp // n_loc
-    base = jnp.zeros((n_exp, 1), jnp.float32)
+    exp_iota = lax.broadcasted_iota(jnp.int32, (LANES, blk), 0)
+    ones = jnp.ones((8, blk), jnp.bfloat16)
+    total = jnp.zeros((8, LANES), jnp.float32)
     for b in range(tokens // blk):
         ids = ids_ref[:, b * blk : (b + 1) * blk]
-        hits = [exp_iota == ids[j : j + 1, :] for j in range(top_k)]
-        any_hit = functools.reduce(jnp.logical_or, hits)
-        hot = jnp.where(any_hit, 1.0, 0.0)
-        rank = jnp.dot(hot.astype(jnp.bfloat16), before, preferred_element_type=jnp.float32) + base
-        base = base + jnp.sum(hot, axis=1, keepdims=True)
-        rows = []
+        below = jnp.zeros((LANES, blk), jnp.float32)
         for j in range(top_k):
-            slot = jnp.sum(jnp.where(hits[j], rank, 0.0), axis=0, keepdims=True).astype(jnp.int32)
-            e = ids[j : j + 1, :]
-            rows.append(jnp.where(slot < cap, (e // n_loc) * GROUP + (e % n_loc) * stride + slot, n_pos * GROUP))
-        dest_ref[:, b * blk : (b + 1) * blk] = jnp.concatenate(rows, axis=0)
-
-
-def list_body(top_k, tokens, fill_ref, dest_ref, list_ref, sem):
-    copy = pltpu.make_async_copy(fill_ref, list_ref, sem)
-    copy.start()
-    copy.wait()
-    unroll = 4
-
-    def step(i, carry):
-        for u in range(unroll):
-            t = i * unroll + u
-            for j in range(top_k):
-                list_ref[dest_ref[j * tokens + t]] = t * top_k + j
-        return carry
-
-    lax.fori_loop(0, tokens // unroll, step, 0)
-
-
-def make_list(expert_idx, cap, stride, n_loc):
+            below = below + jnp.where(ids[j : j + 1, :] < exp_iota, 1.0, 0.0)
+        total = total + lax.dot_general(ones, below.astype(jnp.bfloat16), (((1,), (1,)), ((), ())), preferred_element_type=jnp.float32)
+    out_ref[...] = total.astype(jnp.int32)
+
+
+def make_lists(expert_idx, gate_wt):
     tokens, top_k = expert_idx.shape
-    n_pos = 128 // n_loc
-    dest = pl.pallas_call(
-        functools.partial(route_body, cap, stride, n_loc),
-        out_shape=jax.ShapeDtypeStruct((top_k, tokens), jnp.int32),
-        in_specs=[pl.BlockSpec(memory_space=pltpu.VMEM)],
-        out_specs=pl.BlockSpec(memory_space=pltpu.VMEM),
-        cost_estimate=pl.CostEstimate(flops=4_000_000_000, bytes_accessed=1 << 17, transcendentals=0),
-        name="route",
+    pairs = tokens * top_k
+    starts = pl.pallas_call(
+        starts_body,
+        out_shape=jax.ShapeDtypeStruct((8, LANES), jnp.int32),
+        cost_estimate=pl.CostEstimate(flops=2_000_000_000, bytes_accessed=1 << 17, transcendentals=0),
+        name="starts",
     )(expert_idx.T)
-    size = n_pos * GROUP + 1024
-    fill = jnp.full((size,), tokens * top_k, jnp.int32)
-    return pl.pallas_call(
-        functools.partial(list_body, top_k, tokens),
-        out_shape=jax.ShapeDtypeStruct((size,), jnp.int32),
-        in_specs=[pl.BlockSpec(memory_space=pl.ANY), pl.BlockSpec(memory_space=pltpu.SMEM)],
-        out_specs=pl.BlockSpec(memory_space=pltpu.SMEM),
-        scratch_shapes=[pltpu.SemaphoreType.DMA],
-        cost_estimate=pl.CostEstimate(flops=10_000_000_000, bytes_accessed=1 << 17, transcendentals=0),
-        name="lists",
-    )(fill, dest.reshape(-1))
-
-
-def load_lists(groups_ref, list_ref, gate_ref, lists, gates, sems):
-    copies = [pltpu.make_async_copy(list_ref.at[pl.ds(pl.multiple_of(groups_ref[g] * GROUP, GROUP), GROUP)], lists.at[pl.ds(g * GROUP, GROUP)], sems.at[g]) for g in range(2)]
-    copies.append(pltpu.make_async_copy(gate_ref, gates, sems.at[2]))
+    key = expert_idx.reshape(-1) * pairs + jnp.arange(pairs, dtype=jnp.int32)
+    key, gates = lax.sort((key, gate_wt.reshape(-1)), num_keys=1, is_stable=False)
+    rows = lax.rem(key, pairs) // top_k
+    tail = jnp.full((TAIL - LANES,), pairs, jnp.int32)
+    return jnp.concatenate([rows, starts[0], tail]), jnp.concatenate([gates, jnp.zeros((TAIL,), jnp.float32)])
+
+
+def load_lists(list_ref, gate_ref, lists, gates, sems):
+    copies = [pltpu.make_async_copy(list_ref, lists, sems.at[0]), pltpu.make_async_copy(gate_ref, gates, sems.at[1])]
     for c in copies:
         c.start()
     for c in copies:
         c.wait()
 
 
-def dispatch_body(n_blk, stride, top_k, n_loc, groups_ref, list_ref, gate_ref, x_ref, dy_ref, r_ref, c_ref, lists, gates, rows, tile, sems):
+def expert_span(groups_ref, lists, pairs, cap, n_loc, i):
+    e = groups_ref[i // n_loc] * n_loc + lax.rem(i, n_loc)
+    start = lists[pairs + e]
+    return start, jnp.minimum(lists[pairs + e + 1] - start, cap)
+
+
+def dispatch_body(n_blk, stride, cap, n_loc, pairs, groups_ref, list_ref, gate_ref, x_ref, dy_ref, r_ref, c_ref, lists, gates, rows, tile, sems):
     i = pl.program_id(0)
     tokens, width = x_ref.shape
     parts = width // LANES
@@ -102,8 +71,9 @@
 
     @pl.when(i == 0)
     def _():
-        load_lists(groups_ref, list_ref, gate_ref, lists, gates, sems)
+        load_lists(list_ref, gate_ref, lists, gates, sems)
         rows[pl.ds(tokens * slab, slab), :] = jnp.zeros((slab, LANES), jnp.float32)
+        tile[...] = jnp.zeros_like(tile)
 
         def fill(b, carry):
             t0 = pl.multiple_of(b * 16, 16)
@@ -117,32 +87,33 @@
         lax.fori_loop(0, tokens // 16, fill, 0)
 
     upper = lax.broadcasted_iota(jnp.int32, (slab, LANES), 0) < parts
+    slots = lax.broadcasted_iota(jnp.int32, (stride, LANES), 0)
     for b in range(n_blk):
-        e = i * n_blk + b
-        base = (e // n_loc) * GROUP + (e % n_loc) * stride
-
-        def gather(q, carry, base=base):
+        start, count = expert_span(groups_ref, lists, pairs, cap, n_loc, i * n_blk + b)
+
+        def gather(q, carry, start=start):
+            s0 = q * 16
+            at = start + s0
             for u in range(16):
-                s = q * 16 + u
-                p = lists[base + s]
-                row = rows[pl.ds(pl.multiple_of((p // top_k) * slab, slab), slab), :]
-                tile[pl.ds(s, slab, stride=span), :] = row * jnp.where(upper, 1.0, gates[p])
+                row = rows[pl.ds(pl.multiple_of(lists[at + u] * slab, slab), slab), :]
+                tile[pl.ds(s0 + u, slab, stride=span), :] = row * jnp.where(upper, 1.0, gates[at + u])
             return carry
 
-        lax.fori_loop(0, stride // 16, gather, 0)
+        lax.fori_loop(0, lax.shift_right_logical(count + 15, 4), gather, 0)
+        keep = slots < count
         for k in range(parts):
-            r_ref[b, :, k * LANES : (k + 1) * LANES] = tile[pl.ds(k * span, stride), :].astype(jnp.bfloat16)
-            c_ref[b, :, k * LANES : (k + 1) * LANES] = tile[pl.ds((parts + k) * span, stride), :].astype(jnp.bfloat16)
-
-
-def dispatch(groups, lists, gates, x, dy, stride, top_k, n_loc, n_blk=4):
+            r_ref[b, :, k * LANES : (k + 1) * LANES] = jnp.where(keep, tile[pl.ds(k * span, stride), :], 0.0).astype(jnp.bfloat16)
+            c_ref[b, :, k * LANES : (k + 1) * LANES] = jnp.where(keep, tile[pl.ds((parts + k) * span, stride), :], 0.0).astype(jnp.bfloat16)
+
+
+def dispatch(groups, lists, gates, x, dy, stride, cap, n_loc, n_blk=4):
     tokens, width = x.shape
     slab = 2 * (width // LANES)
     n_mine = 2 * n_loc
     shape = jax.ShapeDtypeStruct((n_mine, stride, width), jnp.bfloat16)
     spec = pl.BlockSpec((n_blk, stride, width), lambda i: (i, 0, 0))
     return pl.pallas_call(
-        functools.partial(dispatch_body, n_blk, stride, top_k, n_loc),
+        functools.partial(dispatch_body, n_blk, stride, cap, n_loc, lists.shape[0] - TAIL),
         grid=(n_mine // n_blk,),
         out_shape=(shape, shape),
         in_specs=[
@@ -154,11 +125,11 @@
         ],
         out_specs=(spec, spec),
         scratch_shapes=[
-            pltpu.SMEM((2 * GROUP,), jnp.int32),
+            pltpu.SMEM(lists.shape, jnp.int32),
             pltpu.SMEM(gates.shape, jnp.float32),
             pltpu.VMEM(((tokens + 1) * slab, LANES), jnp.float32),
             pltpu.VMEM((ceil_to(slab * (stride + 1), 8), LANES), jnp.float32),
-            pltpu.SemaphoreType.DMA((3,)),
+            pltpu.SemaphoreType.DMA((2,)),
         ],
         compiler_params=pltpu.CompilerParams(dimension_semantics=("arbitrary",), vmem_limit_bytes=VMEM_BIG),
         cost_estimate=pl.CostEstimate(flops=10_000_000_000, bytes_accessed=1 << 24, transcendentals=0),
@@ -166,7 +137,7 @@
     )(groups, lists, gates, x, dy)
 
 
-def combine_body(n_blk, stride, top_k, n_loc, groups_ref, list_ref, gate_ref, o_ref, dr_ref, out_ref, lists, gates, acc, tile, sems):
+def combine_body(n_blk, stride, cap, n_loc, pairs, groups_ref, list_ref, gate_ref, o_ref, dr_ref, out_ref, lists, gates, acc, tile, sems):
     i = pl.program_id(0)
     tokens = out_ref.shape[0]
     width = o_ref.shape[-1]
@@ -176,7 +147,7 @@
 
     @pl.when(i == 0)
     def _():
-        load_lists(groups_ref, list_ref, gate_ref, lists, gates, sems)
+        load_lists(list_ref, gate_ref, lists, gates, sems)
 
         def clear(b, carry):
             acc[pl.ds(pl.multiple_of(b * 8 * slab, 8 * slab), 8 * slab), :] = jnp.zeros((8 * slab, LANES), jnp.float32)
@@ -186,27 +157,33 @@
 
     upper = lax.broadcasted_iota(jnp.int32, (slab, LANES), 0) < parts
     for b in range(n_blk):
-        e = i * n_blk + b
-        base = (e // n_loc) * GROUP + (e % n_loc) * stride
+        start, count = expert_span(groups_ref, lists, pairs, cap, n_loc, i * n_blk + b)
         for k in range(parts):
             tile[pl.ds(k * span, stride), :] = o_ref[0, b, :, k * LANES : (k + 1) * LANES].astype(jnp.float32)
             tile[pl.ds((parts + k) * span, stride), :] = dr_ref[0, b, :, k * LANES : (k + 1) * LANES].astype(jnp.float32)
 
-        def scatter(q, carry, base=base):
-            for half in range(2):
-                at, sums = [], []
-                for u in range(8):
-                    s = q * 16 + half * 8 + u
-                    p = lists[base + s]
-                    a = pl.multiple_of((p // top_k) * slab, slab)
-                    row = tile[pl.ds(s, slab, stride=span), :] * jnp.where(upper, gates[p], 1.0)
-                    at.append(a)
-                    sums.append(acc[pl.ds(a, slab), :] + row)
-                for a, v in zip(at, sums):
-                    acc[pl.ds(a, slab), :] = v
+        def scatter(n, limit, s0, start):
+            ats, sums = [], []
+            for u in range(n):
+                at = start + s0 + u
+                t = lists[at] if limit is None else jnp.where(s0 + u < limit, lists[at], tokens)
+                a = pl.multiple_of(t * slab, slab)
+                row = tile[pl.ds(s0 + u, slab, stride=span), :] * jnp.where(upper, gates[at], 1.0)
+                ats.append(a)
+                sums.append(acc[pl.ds(a, slab), :] + row)
+            for a, v in zip(ats, sums):
+                acc[pl.ds(a, slab), :] = v
+
+        def full(q, carry, start=start):
+            scatter(8, None, q * 8, start)
             return carry
 
-        lax.fori_loop(0, stride // 16, scatter, 0)
+        whole = lax.shift_right_logical(count, 3)
+        lax.fori_loop(0, whole, full, 0)
+
+        @pl.when(whole * 8 < count)
+        def _(start=start, count=count, whole=whole):
+            scatter(8, count, whole * 8, start)
 
     @pl.when(i == pl.num_programs(0) - 1)
     def _():
@@ -219,13 +196,13 @@
         lax.fori_loop(0, tokens // 8, write, 0)
 
 
-def combine(block, groups, lists, gates, o, dr, tokens, stride, top_k, n_loc, n_blk=4):
-    width = o.shape[-1]
+def combine(block, groups, lists, gates, o, dr, tokens, cap, n_loc, n_blk=4):
+    stride, width = o.shape[2:]
     slab = 2 * (width // LANES)
     n_mine = 2 * n_loc
     spec = pl.BlockSpec((1, n_blk, stride, width), lambda i: (block, i, 0, 0))
     return pl.pallas_call(
-        functools.partial(combine_body, n_blk, stride, top_k, n_loc),
+        functools.partial(combine_body, n_blk, stride, cap, n_loc, lists.shape[0] - TAIL),
         grid=(n_mine // n_blk,),
         out_shape=jax.ShapeDtypeStruct((tokens, 2 * width), jnp.float32),
         in_specs=[
@@ -237,11 +214,11 @@
         ],
         out_specs=pl.BlockSpec(memory_space=pltpu.VMEM),
         scratch_shapes=[
-            pltpu.SMEM((2 * GROUP,), jnp.int32),
+            pltpu.SMEM(lists.shape, jnp.int32),
             pltpu.SMEM(gates.shape, jnp.float32),
             pltpu.VMEM(((tokens + 1) * slab, LANES), jnp.float32),
             pltpu.VMEM((ceil_to(slab * (stride + 1), 8), LANES), jnp.float32),
-            pltpu.SemaphoreType.DMA((3,)),
+            pltpu.SemaphoreType.DMA((2,)),
         ],
         compiler_params=pltpu.CompilerParams(dimension_semantics=("arbitrary",), vmem_limit_bytes=VMEM_BIG),
         cost_estimate=pl.CostEstimate(flops=14_000_000_000, bytes_accessed=1 << 24, transcendentals=0),
@@ -505,13 +482,12 @@
             four = jnp.stack([v, one, jnp.concatenate([two_a, two_b], axis=0), three])
             held.append(gather_ring(four, last, 2))
 
-        gates = jnp.concatenate([gate_wt.reshape(-1), jnp.zeros((1024,), jnp.float32)])
-        lists = make_list(expert_idx, cap, stride, n_loc)
+        lists, gates = make_lists(expert_idx, gate_wt)
         sets = [(tok_in, grad_out, gates, lists)]
         sets.append(tuple(lax.ppermute(a, "expert", mate) for a in sets[0]))
         sets.append(tuple(lax.ppermute(a, "expert", to_neighbour) for a in sets[0]))
         sets.append(tuple(lax.ppermute(a, "expert", mate) for a in sets[2]))
-        sent = [dispatch(groups, li, g, x, d, stride, top_k, n_loc) for x, d, g, li in sets]
+        sent = [dispatch(groups, li, g, x, d, stride, cap, n_loc) for x, d, g, li in sets]
         r_sets, c_sets = [s[0] for s in sent], [s[1] for s in sent]
 
         prev = None
@@ -530,7 +506,7 @@
                 grads[colour, chunk] = (mine, lax.ppermute(theirs, "expert", partner))
         o_all, dr_all = prev
 
-        sums = [combine(k, groups, sets[k][3], sets[k][2], o_all, dr_all, tokens, stride, top_k, n_loc) for k in (3, 2, 1, 0)][::-1]
+        sums = [combine(k, groups, sets[k][3], sets[k][2], o_all, dr_all, tokens, cap, n_loc) for k in (3, 2, 1, 0)][::-1]
         near = sums[2] + lax.ppermute(sums[3], "expert", mate)
         far = lax.ppermute(near, "expert", to_home)
         total = sums[0] + lax.ppermute(sums[1], "expert", mate) + far

time: 874 us -> 662 us (0.76)
  the two profiles are of different devices: /device:TPU:1 before, /device:TPU:0 now
where the time goes in v2:
time: 662 us; the launch traced here: 651 us
  Pallas kernels  271 us (41%)
  waiting for transfers between devices  204 us (31%)
  starting transfers between devices  88.9 us (13%)
  other arithmetic  69.2 us (10%)
  local copies, waits for them, and re-layouts  16.1 us (2%)
    ppermute x48, waiting for transfers between devices, step_along(): return lax.ppermute(v, 'data', perms[axis](d))  168 us
    pallas_call x4, Pallas kernels, experts(): pl.pallas_call(functools.partial(experts_body, n_sets, last, first, prev...  107 us
    pallas_call x4, Pallas kernels, combine(): pl.pallas_call(functools.partial(combine_body, n_blk, stride, cap, n_loc,...  86.5 us
    pallas_call x4, Pallas kernels, dispatch(): pl.pallas_call(functools.partial(dispatch_body, n_blk, stride, cap, n_loc...  70 us
    ppermute x48, starting transfers between devices, step_along(): return lax.ppermute(v, 'data', perms[axis](d))  67.6 us
    ppermute x4, waiting for transfers between devices, local_step(): lax.ppermute(a, 'expert', to_neighbour)  29.9 us
  transfers between devices with their start and end apart: 68, of which 31 were waited for; matrix products, arithmetic and copies ran while one was open for 10% of the time, Pallas kernels for 26%

profile of v2, /device:TPU:0, one launch (start us, length us, event | category | flops | bytes accessed | tf_op | source)
XLA Modules:
  0.0 651.1 jit_solution(18383039604590243778)
XLA Ops:
  7.6 6.4 sort.15
  15.4 4.1 collective-permute-done.12
  61.5 11.9 %collective-permute-done.6.x_ref = bf16[2048,512]{1,0:T(8,128)(2,1)S(1)} collective-permute-done((bf16[2048,512]{1,0:T(8,128)(2,1)S(1)}, bf16[2048,512]{1,0:T(8,128)(2,1)S(1)}, u32[]{:S(2)}, u32[]{:S(2)}) %collective-permute-start.6) | collective-permute-done | bytes 2097184 | tf_op jit(solution)/shard_map/ppermute | solution.py:488
  77.9 18.0 %collective-permute-done.7.dy_ref = bf16[2048,512]{1,0:T(8,128)(2,1)} collective-permute-done((bf16[2048,512]{1,0:T(8,128)(2,1)}, bf16[2048,512]{1,0:T(8,128)(2,1)}, u32[]{:S(2)}, u32[]{:S(2)}) %collective-permute-start.7) | collective-permute-done | bytes 2097184 | tf_op jit(solution)/shard_map/ppermute | solution.py:488
  96.6 12.8 %collective-permute-done.26.refs_11_ = bf16[4,16,144,128]{3,2,1,0:T(8,128)(2,1)} collective-permute-done((bf16[4,16,144,128]{3,2,1,0:T(8,128)(2,1)}, bf16[4,16,144,128]{3,2,1,0:T(8,128)(2,1)}, u32[]{:S(2)}, u32[]{:S(2)}) %collective-permute-start.26) | collective-permute-done | bytes 2359328 | tf_op jit(solution)/shard_map/ppermute | solution.py:445
  110.5 17.4 %dispatch.4 = (bf16[32,160,512]{2,1,0:T(8,128)(2,1)}, bf16[32,160,512]{2,1,0:T(8,128)(2,1)}) custom-call(s32[2]{0:T(128)} %pad_add_fusion.1.groups_ref, s32[17408]{0:T(1024)} %copy-done.15, f32[17408]{0:T(1024)} %concatenate.51.gate_ref, bf16[2048,512]{1,0:T(8,128)(2,1)} %x_ref.1, bf16[2048,512]{1,0:T(8,128)(2,1)} %dy_ref.1), custom_call_target="tpu_custom_call" | custom-call | flops 10000000000 | bytes 16777216 | tf_op jit(solution)/shard_map/dispatch/pallas_call | solution.py:115
  128.6 17.4 %dispatch.6 = (bf16[32,160,512]{2,1,0:T(8,128)(2,1)}, bf16[32,160,512]{2,1,0:T(8,128)(2,1)}) custom-call(s32[2]{0:T(128)} %pad_add_fusion.1.groups_ref, s32[17408]{0:T(1024)} %copy-done.31, f32[17408]{0:T(1024)} %collective-permute-done.5.gate_ref, bf16[2048,512]{1,0:T(8,128)(2,1)} %copy-done.18, bf16[2048,512]{1,0:T(8,128)(2,1)} %collective-permute-done.7.dy_ref), custom_call_target="tpu_custom_call" | custom-call | flops 10000000000 | bytes 16777216 | tf_op jit(solution)/shard_map/dispatch/pallas_call | solution.py:115
  153.1 17.6 %dispatch.5 = (bf16[32,160,512]{2,1,0:T(8,128)(2,1)}, bf16[32,160,512]{2,1,0:T(8,128)(2,1)}) custom-call(s32[2]{0:T(128)} %pad_add_fusion.1.groups_ref, s32[17408]{0:T(1024)} %collective-permute-done.list_ref, f32[17408]{0:T(1024)} %copy-done.30, bf16[2048,512]{1,0:T(8,128)(2,1)} %copy-done.19, bf16[2048,512]{1,0:T(8,128)(2,1)} %collective-permute-done.3.dy_ref), custom_call_target="tpu_custom_call" | custom-call | flops 10000000000 | bytes 16777216 | tf_op jit(solution)/shard_map/dispatch/pallas_call | solution.py:115
  177.6 17.5 %dispatch.7 = (bf16[32,160,512]{2,1,0:T(8,128)(2,1)}, bf16[32,160,512]{2,1,0:T(8,128)(2,1)}) custom-call(s32[2]{0:T(128)} %pad_add_fusion.1.groups_ref, s32[17408]{0:T(1024)} %collective-permute-done.8.list_ref, f32[17408]{0:T(1024)} %copy-done.33, bf16[2048,512]{1,0:T(8,128)(2,1)} %collective-permute-done.10.x_ref, ...), custom_call_target="tpu_custom_call" | custom-call | flops 10000000000 | bytes 16777216 | tf_op jit(solution)/shard_map/dispatch/pallas_call | solution.py:115
  195.1 26.9 %experts.4 = (bf16[4,32,160,512]{3,2,1,0:T(8,128)(2,1)}, bf16[4,32,160,512]{3,2,1,0:T(8,128)(2,1)}, f32[4,8,144,128]{3,2,1,0:T(8,128)}, f32[4,8,144,128]{3,2,1,0...) custom-call(s32[2]{0:T(128)} %pad_add_fusion.2.refs_0_, ...), custom_call_target="tpu_custom_call" | custom-call | flops 24000000000 | bytes 48000000 | tf_op jit(solution)/shard_map/experts/pallas_call | solution.py:399
  223.4 26.8 %experts.5 = (bf16[4,32,160,512]{3,2,1,0:T(8,128)(2,1)}, bf16[4,32,160,512]{3,2,1,0:T(8,128)(2,1)}, f32[4,8,144,128]{3,2,1,0:T(8,128)}, f32[4,8,144,128]{3,2,1,0...) custom-call(s32[2]{0:T(128)} %pad_add_fusion.2.refs_0_, ...), custom_call_target="tpu_custom_call", output_to_operand_aliasing={{0}: (14, {}), {1}: (15, {})} | custom-call | flops 24000000000 | bytes 48000000 | tf_op jit(solution)/shard_map/experts/pallas_call | solution.py:399
  250.2 26.8 %experts.6 = (bf16[4,32,160,512]{3,2,1,0:T(8,128)(2,1)}, bf16[4,32,160,512]{3,2,1,0:T(8,128)(2,1)}, f32[4,8,144,128]{3,2,1,0:T(8,128)}, f32[4,8,144,128]{3,2,1,0...) custom-call(s32[2]{0:T(128)} %pad_add_fusion.2.refs_0_, ...), custom_call_target="tpu_custom_call", output_to_operand_aliasing={{0}: (14, {}), {1}: (15, {})} | custom-call | flops 24000000000 | bytes 48000000 | tf_op jit(solution)/shard_map/experts/pallas_call | solution.py:399
  277.1 26.9 %experts.7 = (bf16[4,32,160,512]{3,2,1,0:T(8,128)(2,1)}, bf16[4,32,160,512]{3,2,1,0:T(8,128)(2,1)}, f32[4,8,144,128]{3,2,1,0:T(8,128)}, f32[4,8,144,128]{3,2,1,0...) custom-call(s32[2]{0:T(128)} %pad_add_fusion.2.refs_0_, ...), custom_call_target="tpu_custom_call", output_to_operand_aliasing={{0}: (14, {}), {1}: (15, {})} | custom-call | flops 24000000000 | bytes 48000000 | tf_op jit(solution)/shard_map/experts/pallas_call | solution.py:399
  303.9 21.8 %combine.7 = f32[2048,1024]{1,0:T(8,128)} custom-call(s32[2]{0:T(128)} %pad_add_fusion.1.groups_ref, s32[17408]{0:T(1024)} %collective-permute-done.8.list_ref, f32[17408]{0:T(1024)} %copy-done.33, bf16[4,32,160,512]{3,2,1,0:T(8,128)(2,1)} %get-tuple-element.254.o_ref, bf16[4,32,160,512]{3,2,1,0:T(8,128)(2,1)} %get-tuple-element.255.dr_ref), custom_call_target="tpu_custom_call" | custom-call | flops 14000000000 | bytes 16777216 | tf_op jit(solution)/shard_map/combine/pallas_call | solution.py:204
  331.7 23.8 %collective-permute-done.32 = f32[2,8,144,128]{3,2,1,0:T(8,128)S(1)} collective-permute-done((f32[2,8,144,128]{3,2,1,0:T(8,128)}, f32[2,8,144,128]{3,2,1,0:T(8,128)S(1)}, u32[]{:S(2)}, u32[]{:S(2)}) %collective-permute-start.32) | collective-permute-done | bytes 1179680 | tf_op jit(solution)/shard_map/ppermute | solution.py:445
  355.5 3.6 collective-permute-start.52
  361.6 18.4 %collective-permute-done.43 = f32[2,8,144,128]{3,2,1,0:T(8,128)S(1)} collective-permute-done((f32[2,8,144,128]{3,2,1,0:T(8,128)}, f32[2,8,144,128]{3,2,1,0:T(8,128)S(1)}, u32[]{:S(2)}, u32[]{:S(2)}) %collective-permute-start.43) | collective-permute-done | bytes 1179680 | tf_op jit(solution)/shard_map/ppermute | solution.py:445
  397.3 12.3 %collective-permute-done.61 = f32[2,8,144,128]{3,2,1,0:T(8,128)} collective-permute-done((f32[2,8,144,128]{3,2,1,0:T(8,128)S(1)}, f32[2,8,144,128]{3,2,1,0:T(8,128)}, u32[]{:S(2)}, u32[]{:S(2)}) %collective-permute-start.61) | collective-permute-done | bytes 1179680 | tf_op jit(solution)/shard_map/ppermute | solution.py:445
  409.6 3.7 collective-permute-start.53
  416.0 21.5 %combine.6 = f32[2048,1024]{1,0:T(8,128)} custom-call(s32[2]{0:T(128)} %pad_add_fusion.1.groups_ref, s32[17408]{0:T(1024)} %copy-done.31, f32[17408]{0:T(1024)} %collective-permute-done.5.gate_ref, bf16[4,32,160,512]{3,2,1,0:T(8,128)(2,1)} %get-tuple-element.254.o_ref, bf16[4,32,160,512]{3,2,1,0:T(8,128)(2,1)} %get-tuple-element.255.dr_ref), custom_call_target="tpu_custom_call" | custom-call | flops 14000000000 | bytes 16777216 | tf_op jit(solution)/shard_map/combine/pallas_call | solution.py:204
  437.5 21.6 %combine.5 = f32[2048,1024]{1,0:T(8,128)} custom-call(s32[2]{0:T(128)} %pad_add_fusion.1.groups_ref, s32[17408]{0:T(1024)} %collective-permute-done.list_ref, f32[17408]{0:T(1024)} %copy-done.30, bf16[4,32,160,512]{3,2,1,0:T(8,128)(2,1)} %get-tuple-element.254.o_ref, bf16[4,32,160,512]{3,2,1,0:T(8,128)(2,1)} %get-tuple-element.255.dr_ref), custom_call_target="tpu_custom_call" | custom-call | flops 14000000000 | bytes 16777216 | tf_op jit(solution)/shard_map/combine/pallas_call | solution.py:204
  459.2 12.3 %add.341 = f32[2048,1024]{1,0:T(8,128)} add(f32[2048,1024]{1,0:T(8,128)} %combine.6, f32[2048,1024]{1,0:T(8,128)} %collective-permute-done.30) | non-fusion elementwise | flops 2097152 | bytes 25165824 | tf_op jit(solution)/shard_map/add | solution.py:510
  481.0 14.5 %collective-permute-done.44 = f32[4,8,144,128]{3,2,1,0:T(8,128)} collective-permute-done((f32[4,8,144,128]{3,2,1,0:T(8,128)}, f32[4,8,144,128]{3,2,1,0:T(8,128)}, u32[]{:S(2)}, u32[]{:S(2)}) %collective-permute-start.44) | collective-permute-done | bytes 2359328 | tf_op jit(solution)/shard_map/ppermute | solution.py:445
  500.8 28.3 %collective-permute-done.42 = f32[4,8,144,128]{3,2,1,0:T(8,128)S(1)} collective-permute-done((f32[4,8,144,128]{3,2,1,0:T(8,128)S(1)}, f32[4,8,144,128]{3,2,1,0:T(8,128)S(1)}, u32[]{:S(2)}, u32[]{:S(2)}) %collective-permute-start.42) | collective-permute-done | bytes 2359328 | tf_op jit(solution)/shard_map/ppermute | solution.py:445
  531.2 3.5 collective-permute-start.38
  534.7 16.1 %collective-permute-done.60 = f32[4,8,144,128]{3,2,1,0:T(8,128)S(1)} collective-permute-done((f32[4,8,144,128]{3,2,1,0:T(8,128)S(1)}, f32[4,8,144,128]{3,2,1,0:T(8,128)S(1)}, u32[]{:S(2)}, u32[]{:S(2)}) %collective-permute-start.60) | collective-permute-done | bytes 2359328 | tf_op jit(solution)/shard_map/ppermute | solution.py:445
  562.4 3.9 collective-permute-done.45
  570.6 4.6 collective-permute-done.65
  585.8 4.7 collective-permute-done.55
  610.2 21.6 %combine.4 = f32[2048,1024]{1,0:T(8,128)} custom-call(s32[2]{0:T(128)} %pad_add_fusion.1.groups_ref, s32[17408]{0:T(1024)} %copy-done.15, f32[17408]{0:T(1024)} %concatenate.51.gate_ref, bf16[4,32,160,512]{3,2,1,0:T(8,128)(2,1)} %get-tuple-element.254.o_ref, bf16[4,32,160,512]{3,2,1,0:T(8,128)(2,1)} %get-tuple-element.255.dr_ref), custom_call_target="tpu_custom_call" | custom-call | flops 14000000000 | bytes 16777216 | tf_op jit(solution)/shard_map/combine/pallas_call | solution.py:204
  635.6 9.9 %add_add_fusion = f32[2048,1024]{1,0:T(8,128)S(1)} fusion(f32[2048,1024]{1,0:T(8,128)} %collective-permute-done.31, f32[2048,1024]{1,0:T(8,128)} %combine.4, f32[2048,1024]{1,0:T(8,128)} %collective-permute-done.29), kind=kLoop, calls=%fused_computation | loop fusion | flops 4194304 | bytes 33554432 | tf_op jit(solution)/shard_map/add | solution.py:512
  645.5 5.1 fusion
  (256 shorter events, 167.3 us)
Async XLA Ops:
  14.7 31.4 %collective-permute-start.5 = (f32[17408]{0:T(1024)}, f32[17408]{0:T(1024)}, u32[]{:S(2)}, u32[]{:S(2)}) collective-permute-start(f32[17408]{0:T(1024)} %concatenate.51.gate_ref), channel_id=1, source_target_pairs={{0,2},{1,7},{2,4},{3,1},{4,6},{5,3},{6,0},{7,5},{8,10},{9,15},{10,... | collective-permute-start | bytes 208904 | tf_op jit(solution)/shard_map/ppermute | solution.py:488
  54.5 54.9 %collective-permute-start.26 = (bf16[4,16,144,128]{3,2,1,0:T(8,128)(2,1)}, bf16[4,16,144,128]{3,2,1,0:T(8,128)(2,1)}, u32[]{:S(2)}, u32[]{:S(2)}) collective-permute-start(bf16[4,16,144,128]{3,2,1,0:T(8,128)(2,1)} %pad_maximum_fusion.1.refs_9_), channel_id=1, source_target_pairs={{0,96},{8,104},{16,112},{24,120},{32,0},{40,8},{48,16},{56,24},{64... | collective-permute-start | bytes 7077896 | tf_op jit(solution)/shard_map/ppermute | solution.py:445
  56.3 54.2 %collective-permute-start.25 = (bf16[4,16,144,128]{3,2,1,0:T(8,128)(2,1)}, bf16[4,16,144,128]{3,2,1,0:T(8,128)(2,1)}, u32[]{:S(2)}, u32[]{:S(2)}) collective-permute-start(bf16[4,16,144,128]{3,2,1,0:T(8,128)(2,1)} %pad_maximum_fusion.1.refs_9_), channel_id=1, source_target_pairs={{0,32},{8,40},{16,48},{24,56},{32,64},{40,72},{48,80},{56,88},{64,... | collective-permute-start | bytes 7077896 | tf_op jit(solution)/shard_map/ppermute | solution.py:445
  59.2 36.7 %collective-permute-start.7 = (bf16[2048,512]{1,0:T(8,128)(2,1)}, bf16[2048,512]{1,0:T(8,128)(2,1)}, u32[]{:S(2)}, u32[]{:S(2)}) collective-permute-start(bf16[2048,512]{1,0:T(8,128)(2,1)} %dy_ref.1), channel_id=1, source_target_pairs={{0,2},{1,7},{2,4},{3,1},{4,6},{5,3},{6,0},{7,5},{8,10},{9,15},{10,... | collective-permute-start | bytes 6291464 | tf_op jit(solution)/shard_map/ppermute | solution.py:488
  73.4 77.0 %collective-permute-start.18 = (bf16[4,16,144,128]{3,2,1,0:T(8,128)(2,1)S(1)}, bf16[4,16,144,128]{3,2,1,0:T(8,128)(2,1)}, u32[]{:S(2)}, u32[]{:S(2)}) collective-permute-start(bf16[4,16,144,128]{3,2,1,0:T(8,128)(2,1)S(1)} %pad_maximum_fusion.refs_9_), channel_id=1, source_target_pairs={{0,24},{8,0},{16,8},{24,16},{32,56},{40,32},{48,40},{56,48},{64,88... | collective-permute-start | bytes 7077896 | tf_op jit(solution)/shard_map/ppermute | solution.py:445
  76.6 76.5 %collective-permute-start.17 = (bf16[4,16,144,128]{3,2,1,0:T(8,128)(2,1)S(1)}, bf16[4,16,144,128]{3,2,1,0:T(8,128)(2,1)}, u32[]{:S(2)}, u32[]{:S(2)}) collective-permute-start(bf16[4,16,144,128]{3,2,1,0:T(8,128)(2,1)S(1)} %pad_maximum_fusion.refs_9_), channel_id=1, source_target_pairs={{0,8},{8,16},{16,24},{24,0},{32,40},{40,48},{48,56},{56,32},{64,72... | collective-permute-start | bytes 7077896 | tf_op jit(solution)/shard_map/ppermute | solution.py:445
  95.9 53.9 %collective-permute-start.3 = (bf16[2048,512]{1,0:T(8,128)(2,1)}, bf16[2048,512]{1,0:T(8,128)(2,1)}, u32[]{:S(2)}, u32[]{:S(2)}) collective-permute-start(bf16[2048,512]{1,0:T(8,128)(2,1)} %dy_ref.1), channel_id=1, source_target_pairs={{0,1},{1,0},{2,3},{3,2},{4,5},{5,4},{6,7},{7,6},{8,9},{9,8},{10,11... | collective-permute-start | bytes 6291464 | tf_op jit(solution)/shard_map/ppermute | solution.py:487
  109.4 67.9 %collective-permute-start.10 = (bf16[2048,512]{1,0:T(8,128)(2,1)}, bf16[2048,512]{1,0:T(8,128)(2,1)}, u32[]{:S(2)}, u32[]{:S(2)}) collective-permute-start(bf16[2048,512]{1,0:T(8,128)(2,1)} %copy-done.18), channel_id=1, source_target_pairs={{0,1},{1,0},{2,3},{3,2},{4,5},{5,4},{6,7},{7,6},{8,9},{9,8},{10,11... | collective-permute-start | bytes 6291464 | tf_op jit(solution)/shard_map/ppermute | solution.py:489
  110.5 67.1 %collective-permute-start.11 = (bf16[2048,512]{1,0:T(8,128)(2,1)}, bf16[2048,512]{1,0:T(8,128)(2,1)}, u32[]{:S(2)}, u32[]{:S(2)}) collective-permute-start(bf16[2048,512]{1,0:T(8,128)(2,1)} %collective-permute-done.7.dy_ref), channel_id=1, source_target_pairs={{0,1},{1,0},{2,3},{3,2},{4,5},{5,4},{6,7},{7,6},{8,9},{9,8},{10,11... | collective-permute-start | bytes 6291464 | tf_op jit(solution)/shard_map/ppermute | solution.py:489
  150.5 44.6 %collective-permute-start.28 = (bf16[2,16,144,128]{3,2,1,0:T(8,128)(2,1)}, bf16[2,16,144,128]{3,2,1,0:T(8,128)(2,1)}, u32[]{:S(2)}, u32[]{:S(2)}) collective-permute-start(bf16[2,16,144,128]{3,2,1,0:T(8,128)(2,1)} %slice.903), channel_id=1, source_target_pairs={{0,96},{8,104},{16,112},{24,120},{32,0},{40,8},{48,16},{56,24},{64... | collective-permute-start | bytes 3538952 | tf_op jit(solution)/shard_map/ppermute | solution.py:445
  153.1 42.1 %collective-permute-start.27 = (bf16[2,16,144,128]{3,2,1,0:T(8,128)(2,1)S(1)}, bf16[2,16,144,128]{3,2,1,0:T(8,128)(2,1)}, u32[]{:S(2)}, u32[]{:S(2)}) collective-permute-start(bf16[2,16,144,128]{3,2,1,0:T(8,128)(2,1)S(1)} %slice.902), channel_id=1, source_target_pairs={{0,32},{8,40},{16,48},{24,56},{32,64},{40,72},{48,80},{56,88},{64,... | collective-permute-start | bytes 3538952 | tf_op jit(solution)/shard_map/ppermute | solution.py:445
  175.4 46.6 %collective-permute-start.20 = (bf16[2,16,144,128]{3,2,1,0:T(8,128)(2,1)}, bf16[2,16,144,128]{3,2,1,0:T(8,128)(2,1)S(1)}, u32[]{:S(2)}, u32[]{:S(2)}) collective-permute-start(bf16[2,16,144,128]{3,2,1,0:T(8,128)(2,1)} %slice.897), channel_id=1, source_target_pairs={{0,24},{8,0},{16,8},{24,16},{32,56},{40,32},{48,40},{56,48},{64,88... | collective-permute-start | bytes 3538952 | tf_op jit(solution)/shard_map/ppermute | solution.py:445
  177.3 44.7 %collective-permute-start.19 = (bf16[2,16,144,128]{3,2,1,0:T(8,128)(2,1)}, bf16[2,16,144,128]{3,2,1,0:T(8,128)(2,1)S(1)}, u32[]{:S(2)}, u32[]{:S(2)}) collective-permute-start(bf16[2,16,144,128]{3,2,1,0:T(8,128)(2,1)} %slice.896), channel_id=1, source_target_pairs={{0,8},{8,16},{16,24},{24,0},{32,40},{40,48},{48,56},{56,32},{64,72... | collective-permute-start | bytes 3538952 | tf_op jit(solution)/shard_map/ppermute | solution.py:445
  325.8 88.2 %collective-permute-start.30 = (f32[2048,1024]{1,0:T(8,128)}, f32[2048,1024]{1,0:T(8,128)}, u32[]{:S(2)}, u32[]{:S(2)}) collective-permute-start(f32[2048,1024]{1,0:T(8,128)} %combine.7), channel_id=1, source_target_pairs={{0,1},{1,0},{2,3},{3,2},{4,5},{5,4},{6,7},{7,6},{8,9},{9,8},{10,11... | collective-permute-start | bytes 25165832 | tf_op jit(solution)/shard_map/ppermute | solution.py:510
  326.0 35.6 %collective-permute-start.34 = (f32[2,8,144,128]{3,2,1,0:T(8,128)S(1)}, f32[2,8,144,128]{3,2,1,0:T(8,128)S(1)}, u32[]{:S(2)}, u32[]{:S(2)}) collective-permute-start(f32[2,8,144,128]{3,2,1,0:T(8,128)S(1)} %copy-done.25), channel_id=1, source_target_pairs={{0,24},{8,0},{16,8},{24,16},{32,56},{40,32},{48,40},{56,48},{64,88... | collective-permute-start | bytes 3538952 | tf_op jit(solution)/shard_map/ppermute | solution.py:445
  329.2 50.8 %collective-permute-start.43 = (f32[2,8,144,128]{3,2,1,0:T(8,128)}, f32[2,8,144,128]{3,2,1,0:T(8,128)S(1)}, u32[]{:S(2)}, u32[]{:S(2)}) collective-permute-start(f32[2,8,144,128]{3,2,1,0:T(8,128)} %get-tuple-element.265), channel_id=1, source_target_pairs={{0,24},{8,0},{16,8},{24,16},{32,56},{40,32},{48,40},{56,48},{64,88... | collective-permute-start | bytes 3538952 | tf_op jit(solution)/shard_map/ppermute | solution.py:445
  331.1 52.3 %collective-permute-start.50 = (f32[2,8,144,128]{3,2,1,0:T(8,128)S(1)}, f32[2,8,144,128]{3,2,1,0:T(8,128)S(1)}, u32[]{:S(2)}, u32[]{:S(2)}) collective-permute-start(f32[2,8,144,128]{3,2,1,0:T(8,128)S(1)} %copy-done.24), channel_id=1, source_target_pairs={{0,32},{8,40},{16,48},{24,56},{32,64},{40,72},{48,80},{56,88},{64,... | collective-permute-start | bytes 3538952 | tf_op jit(solution)/shard_map/ppermute | solution.py:445
  355.5 37.3 %collective-permute-start.52 = (f32[2,8,144,128]{3,2,1,0:T(8,128)S(1)}, f32[2,8,144,128]{3,2,1,0:T(8,128)S(1)}, u32[]{:S(2)}, u32[]{:S(2)}) collective-permute-start(f32[2,8,144,128]{3,2,1,0:T(8,128)S(1)} %copy-done.21), channel_id=1, source_target_pairs={{0,96},{8,104},{16,112},{24,120},{32,0},{40,8},{48,16},{56,24},{64... | collective-permute-start | bytes 3538952 | tf_op jit(solution)/shard_map/ppermute | solution.py:445
  361.6 35.5 %collective-permute-start.59 = (f32[2,8,144,128]{3,2,1,0:T(8,128)S(1)}, f32[2,8,144,128]{3,2,1,0:T(8,128)S(1)}, u32[]{:S(2)}, u32[]{:S(2)}) collective-permute-start(f32[2,8,144,128]{3,2,1,0:T(8,128)S(1)} %copy-done.23), channel_id=1, source_target_pairs={{0,32},{8,40},{16,48},{24,56},{32,64},{40,72},{48,80},{56,88},{64,... | collective-permute-start | bytes 3538952 | tf_op jit(solution)/shard_map/ppermute | solution.py:445
  380.0 29.6 %collective-permute-start.61 = (f32[2,8,144,128]{3,2,1,0:T(8,128)S(1)}, f32[2,8,144,128]{3,2,1,0:T(8,128)}, u32[]{:S(2)}, u32[]{:S(2)}) collective-permute-start(f32[2,8,144,128]{3,2,1,0:T(8,128)S(1)} %copy-done.22), channel_id=1, source_target_pairs={{0,96},{8,104},{16,112},{24,120},{32,0},{40,8},{48,16},{56,24},{64... | collective-permute-start | bytes 3538952 | tf_op jit(solution)/shard_map/ppermute | solution.py:445
  383.4 30.5 %collective-permute-start.41 = (f32[2,8,144,128]{3,2,1,0:T(8,128)S(1)}, f32[2,8,144,128]{3,2,1,0:T(8,128)}, u32[]{:S(2)}, u32[]{:S(2)}) collective-permute-start(f32[2,8,144,128]{3,2,1,0:T(8,128)S(1)} %copy-done.20), channel_id=1, source_target_pairs={{0,8},{8,16},{16,24},{24,0},{32,40},{40,48},{48,56},{56,32},{64,72... | collective-permute-start | bytes 3538952 | tf_op jit(solution)/shard_map/ppermute | solution.py:445
  392.8 78.7 %collective-permute-start.35 = (f32[4,8,144,128]{3,2,1,0:T(8,128)}, f32[4,8,144,128]{3,2,1,0:T(8,128)S(1)}, u32[]{:S(2)}, u32[]{:S(2)}) collective-permute-start(f32[4,8,144,128]{3,2,1,0:T(8,128)} %add_dynamic-update-slice_fusion.6), channel_id=1, source_target_pairs={{0,24},{8,0},{16,8},{24,16},{32,56},{40,32},{48,40},{56,48},{64,88... | collective-permute-start | bytes 7077896 | tf_op jit(solution)/shard_map/ppermute | solution.py:445
  397.1 74.4 %collective-permute-start.33 = (f32[4,8,144,128]{3,2,1,0:T(8,128)}, f32[4,8,144,128]{3,2,1,0:T(8,128)}, u32[]{:S(2)}, u32[]{:S(2)}) collective-permute-start(f32[4,8,144,128]{3,2,1,0:T(8,128)} %add_dynamic-update-slice_fusion.7), channel_id=1, source_target_pairs={{0,8},{8,16},{16,24},{24,0},{32,40},{40,48},{48,56},{56,32},{64,72... | collective-permute-start | bytes 7077896 | tf_op jit(solution)/shard_map/ppermute | solution.py:445
  409.6 66.0 %collective-permute-start.53 = (f32[4,8,144,128]{3,2,1,0:T(8,128)}, f32[4,8,144,128]{3,2,1,0:T(8,128)}, u32[]{:S(2)}, u32[]{:S(2)}) collective-permute-start(f32[4,8,144,128]{3,2,1,0:T(8,128)} %add_dynamic-update-slice_fusion.2), channel_id=1, source_target_pairs={{0,96},{8,104},{16,112},{24,120},{32,0},{40,8},{48,16},{56,24},{64... | collective-permute-start | bytes 7077896 | tf_op jit(solution)/shard_map/ppermute | solution.py:445
  414.0 63.4 %collective-permute-start.51 = (f32[4,8,144,128]{3,2,1,0:T(8,128)}, f32[4,8,144,128]{3,2,1,0:T(8,128)}, u32[]{:S(2)}, u32[]{:S(2)}) collective-permute-start(f32[4,8,144,128]{3,2,1,0:T(8,128)} %add_dynamic-update-slice_fusion.3), channel_id=1, source_target_pairs={{0,32},{8,40},{16,48},{24,56},{32,64},{40,72},{48,80},{56,88},{64,... | collective-permute-start | bytes 7077896 | tf_op jit(solution)/shard_map/ppermute | solution.py:445
  414.0 81.5 %collective-permute-start.44 = (f32[4,8,144,128]{3,2,1,0:T(8,128)}, f32[4,8,144,128]{3,2,1,0:T(8,128)}, u32[]{:S(2)}, u32[]{:S(2)}) collective-permute-start(f32[4,8,144,128]{3,2,1,0:T(8,128)} %add_dynamic-update-slice_fusion.4), channel_id=1, source_target_pairs={{0,24},{8,0},{16,8},{24,16},{32,56},{40,32},{48,40},{56,48},{64,88... | collective-permute-start | bytes 7077896 | tf_op jit(solution)/shard_map/ppermute | solution.py:445
  471.5 164.2 %collective-permute-start.29 = (f32[2048,1024]{1,0:T(8,128)}, f32[2048,1024]{1,0:T(8,128)}, u32[]{:S(2)}, u32[]{:S(2)}) collective-permute-start(f32[2048,1024]{1,0:T(8,128)} %combine.5), channel_id=1, source_target_pairs={{0,1},{1,0},{2,3},{3,2},{4,5},{5,4},{6,7},{7,6},{8,9},{9,8},{10,11... | collective-permute-start | bytes 25165832 | tf_op jit(solution)/shard_map/ppermute | solution.py:512
  471.5 164.2 %collective-permute-start.31 = (f32[2048,1024]{1,0:T(8,128)}, f32[2048,1024]{1,0:T(8,128)}, u32[]{:S(2)}, u32[]{:S(2)}) collective-permute-start(f32[2048,1024]{1,0:T(8,128)} %add.341), channel_id=1, source_target_pairs={{2,0},{7,1},{4,2},{1,3},{6,4},{3,5},{0,6},{5,7},{10,8},{15,9},{12,... | collective-permute-start | bytes 25165832 | tf_op jit(solution)/shard_map/ppermute | solution.py:511
  475.6 53.5 %collective-permute-start.42 = (f32[4,8,144,128]{3,2,1,0:T(8,128)S(1)}, f32[4,8,144,128]{3,2,1,0:T(8,128)S(1)}, u32[]{:S(2)}, u32[]{:S(2)}) collective-permute-start(f32[4,8,144,128]{3,2,1,0:T(8,128)S(1)} %add_dynamic-update-slice_fusion.5), channel_id=1, source_target_pairs={{0,8},{8,16},{16,24},{24,0},{32,40},{40,48},{48,56},{56,32},{64,72... | collective-permute-start | bytes 7077896 | tf_op jit(solution)/shard_map/ppermute | solution.py:445
  477.4 53.8 %collective-permute-start.62 = (f32[4,8,144,128]{3,2,1,0:T(8,128)S(1)}, f32[4,8,144,128]{3,2,1,0:T(8,128)S(1)}, u32[]{:S(2)}, u32[]{:S(2)}) collective-permute-start(f32[4,8,144,128]{3,2,1,0:T(8,128)S(1)} %add_dynamic-update-slice_fusion), channel_id=1, source_target_pairs={{0,96},{8,104},{16,112},{24,120},{32,0},{40,8},{48,16},{56,24},{64... | collective-permute-start | bytes 7077896 | tf_op jit(solution)/shard_map/ppermute | solution.py:445
  495.5 55.3 %collective-permute-start.60 = (f32[4,8,144,128]{3,2,1,0:T(8,128)S(1)}, f32[4,8,144,128]{3,2,1,0:T(8,128)S(1)}, u32[]{:S(2)}, u32[]{:S(2)}) collective-permute-start(f32[4,8,144,128]{3,2,1,0:T(8,128)S(1)} %add_dynamic-update-slice_fusion.1), channel_id=1, source_target_pairs={{0,32},{8,40},{16,48},{24,56},{32,64},{40,72},{48,80},{56,88},{64,... | collective-permute-start | bytes 7077896 | tf_op jit(solution)/shard_map/ppermute | solution.py:445
  600.3 31.5 %collective-permute-start.58 = (f32[4,144,128]{2,1,0:T(8,128)S(1)}, f32[4,144,128]{2,1,0:T(8,128)S(1)}, u32[]{:S(2)}, u32[]{:S(2)}) collective-permute-start(f32[4,144,128]{2,1,0:T(8,128)S(1)} %get-tuple-element.299), channel_id=1, source_target_pairs={{0,4},{1,5},{2,6},{3,7},{4,0},{5,1},{6,2},{7,3},{8,12},{9,13},{10,... | collective-permute-start | bytes 884744 | tf_op jit(solution)/shard_map/ppermute | solution.py:506
  (70 other events, 1041.8 us)
